TPU v7x, 256 devices: a whole 4x4x8 slice. The times are simulated.
256 devices in a mesh: gx: 32 (over z_hi, y, core), gy: 8 (over x, z_lo).
Axes of the slice: x: 4, y: 4, z: 8 (z_hi: 4, z_lo: 2; z = z_hi * 2 + z_lo), core: 2. Of those that a mesh axis runs over, the one named last changes fastest.
Arguments:
- state: float32 [12, 256, 16, 2048], P(None, 'gx', None, 'gy'), may hold values from -0.9 to 1, as said below
- tissue_mask: int32 [256, 16, 16], P('gx', None, 'gy'), may hold values 0 or 1
- layer_index: int32 [16], replicated, may hold values from 0 to 7
- fibre: float32 [2, 8], replicated, may hold values from -1.2 to 1.2
Outputs:
- new_state: float32 [12, 256, 16, 2048], P(None, 'gx', None, 'gy')
Inputs may be any that keep to these rules, and one draw needn't show every extreme that they name: `state`: component 0 lies within -0.9 to 0.3, components 1 to 10 within 0 to 1, component 11 within 0.05 to 1.
All inputs are finite; a program needn't handle non-finite values.
Results may differ from a plain program's by a relative error of at most 0.00002.
Values sent between devices are 32-bit elements.
A program may use at most 64 MiB of HBM per device.

v0:
```python
import math

import jax
import jax.numpy as jnp
from jax import lax
from jax.sharding import PartitionSpec as P

STEPS = 8
MASK_BLOCK = 128


time_step = 0.02
thermal_volt = 8314.472 * 310.0 / 96485.3415
potassium_out = 5.4
sodium_out = 140.0
calcium_out = 2.0
potassium_in = 138.3
sodium_in = 7.67
transverse = 0.04
longitudinal = 0.12


def padded(x, sides, width):
    for axis, dim in sides:
        size, length = (lax.axis_size(axis), x.shape[dim])
        up = [(i, (i + 1) % size) for i in range(size - 1)]
        down = [(j, i) for i, j in up]
        last = lax.slice_in_dim(x, length - width, length, axis=dim)
        leading = lax.slice_in_dim(x, 0, width, axis=dim)
        before = lax.ppermute(last, axis, up)
        after = lax.ppermute(leading, axis, down)
        x = jnp.concatenate([before, x, after], axis=dim)
    return x


def settle(gate, steady, tau):
    return steady + (gate - steady) * jnp.exp(-time_step / tau)


def settle_rate(gate, steady, rate):
    return steady + (gate - steady) * jnp.exp(-time_step * rate)


def membrane(state):
    sig = jax.nn.sigmoid
    voltage = 100.0 * state[0]
    sodium_act = state[1]
    sodium_inact = state[2]
    sodium_slow = state[3]
    calcium_act = state[4]
    calcium_inact = state[5]
    transient_act = state[6]
    transient_inact = state[7]
    rapid_act = state[8]
    rapid_inact = state[9]
    slow_act = state[10]
    calcium = state[11]
    calcium_mm = jnp.maximum(calcium, 0.02) * 0.001
    rev_potassium = thermal_volt * math.log(potassium_out / potassium_in)
    rev_sodium = thermal_volt * math.log(sodium_out / sodium_in)
    rev_slow = thermal_volt * math.log(
        (potassium_out + 0.03 * sodium_out) / (potassium_in + 0.03 * sodium_in)
    )
    rev_calcium = 0.5 * thermal_volt * jnp.log(calcium_out / calcium_mm)
    sodium_current = 14.838 * sodium_act**3 * sodium_inact * sodium_slow * (voltage - rev_sodium)
    calcium_current = 0.08 * calcium_act * calcium_inact * (voltage - rev_calcium)
    transient_current = 0.294 * transient_act * transient_inact * (voltage - rev_potassium)
    rapid_current = 0.153 * rapid_act * rapid_inact * (voltage - rev_potassium)
    slow_current = 0.392 * slow_act**2 * (voltage - rev_slow)
    above = voltage - rev_potassium
    alpha_inward = 0.1 * sig(-0.06 * (above - 200.0))
    beta_inward = (3.0 * jnp.exp(0.0002 * (above + 100.0)) + jnp.exp(0.1 * (above - 10.0))) * sig(
        0.5 * above
    )
    inward_current = 5.405 * alpha_inward / (alpha_inward + beta_inward) * above
    plateau_current = 0.0146 * sig((voltage - 25.0) / 5.98) * above
    scaled = voltage / thermal_volt
    pump_current = (
        2.724
        * potassium_out
        / (potassium_out + 1.0)
        * sodium_in
        / (sodium_in + 40.0)
        / (1.0 + 0.1245 * jnp.exp(-0.1 * scaled) + 0.0353 * jnp.exp(-scaled))
    )
    exchange_current = (
        1000.0
        * (
            jnp.exp(0.35 * scaled) * sodium_in**3 * calcium_out
            - 2.5 * jnp.exp(-0.65 * scaled) * sodium_out**3 * calcium_mm
        )
        / ((87.5**3 + sodium_out**3) * (1.38 + calcium_out) * (1.0 + 0.1 * jnp.exp(-0.65 * scaled)))
    )
    pump_calcium = 0.1238 * calcium_mm / (calcium_mm + 0.0005)
    back_sodium = 0.00029 * (voltage - rev_sodium)
    back_calcium = 0.000592 * (voltage - rev_calcium)
    ionic_total = (
        sodium_current
        + calcium_current
        + transient_current
        + rapid_current
        + slow_current
        + inward_current
        + plateau_current
        + pump_current
        + exchange_current
        + pump_calcium
        + back_sodium
        + back_calcium
    )
    new_voltage = voltage - time_step * ionic_total
    new_calcium = calcium - time_step * 0.05 * (
        calcium_current + back_calcium + pump_calcium - 2.0 * exchange_current
    )
    upper = sig((voltage + 40.0) / 2.0)
    lower = sig(-(voltage + 40.0) / 2.0)
    tau_act = sig((voltage + 60.0) / 5.0) * (
        0.1 * sig(-(voltage + 35.0) / 5.0) + 0.1 * sig(-(voltage - 50.0) / 200.0)
    )
    new_act = settle(sodium_act, sig((voltage + 56.86) / 9.03) ** 2, tau_act)
    inact_steady = sig(-(voltage + 71.55) / 7.43) ** 2
    rate_inact = (
        lower * 0.057 * jnp.exp(-(voltage + 80.0) / 6.8)
        + upper * (0.77 / 0.13) * sig((voltage + 10.66) / 11.1)
        + lower * (2.7 * jnp.exp(0.079 * voltage) + 310000.0 * jnp.exp(0.3485 * voltage))
    )
    new_inact = settle_rate(sodium_inact, inact_steady, rate_inact)
    rate_slow = (
        lower
        * (-25428.0 * jnp.exp(0.2444 * voltage) - 6.948e-06 * jnp.exp(-0.04391 * voltage))
        * (voltage + 37.78)
        * sig(-0.311 * (voltage + 79.23))
        + lower * 0.02424 * jnp.exp(-0.01052 * voltage) * sig(0.1378 * (voltage + 40.14))
        + upper * 0.6 * jnp.exp(0.057 * voltage) * sig(0.1 * (voltage + 32.0))
    )
    new_slow = settle_rate(sodium_slow, inact_steady, rate_slow)
    tau_calact = (1.4 * sig((voltage + 35.0) / 13.0) + 0.25) * 1.4 * sig(
        -(voltage + 5.0) / 5.0
    ) + sig((voltage - 50.0) / 20.0)
    new_calact = settle(calcium_act, sig((voltage + 8.0) / 7.5), tau_calact)
    tau_calinact = (
        1102.5 * jnp.exp(-((voltage + 27.0) ** 2) / 225.0)
        + 200.0 * sig((voltage - 13.0) / 10.0)
        + 180.0 * sig(-(voltage + 30.0) / 10.0)
        + 20.0
    )
    new_calinact = settle(calcium_inact, sig(-(voltage + 20.0) / 7.0), tau_calinact)
    tau_tract = 9.5 * jnp.exp(-((voltage + 40.0) ** 2) / 1800.0) + 0.8
    new_tract = settle(transient_act, sig((voltage - 20.0) / 6.0), tau_tract)
    tau_trinact = (
        85.0 * jnp.exp(-((voltage + 45.0) ** 2) / 320.0) + 5.0 * sig(-(voltage - 20.0) / 5.0) + 3.0
    )
    new_trinact = settle(transient_inact, sig(-(voltage + 20.0) / 5.0), tau_trinact)
    tau_rapact = 450.0 * sig((voltage + 45.0) / 10.0) * 6.0 * sig(-(voltage + 30.0) / 11.5)
    new_rapact = settle(rapid_act, sig((voltage + 26.0) / 7.0), tau_rapact)
    tau_rapinact = 3.0 * sig((voltage + 60.0) / 20.0) * 1.12 * sig(-(voltage - 60.0) / 20.0)
    new_rapinact = settle(rapid_inact, sig(-(voltage + 88.0) / 24.0), tau_rapinact)
    tau_slowact = (
        1400.0 * jnp.sqrt(sig((voltage - 5.0) / 6.0)) * sig(-(voltage - 35.0) / 15.0) + 80.0
    )
    new_slowact = settle(slow_act, sig((voltage + 5.0) / 14.0), tau_slowact)
    return jnp.stack(
        [
            new_voltage / 100.0,
            new_act,
            new_inact,
            new_slow,
            new_calact,
            new_calinact,
            new_tract,
            new_trinact,
            new_rapact,
            new_rapinact,
            new_slowact,
            new_calcium,
        ]
    )


def advance(state, inside):
    return jnp.where(inside[None], membrane(state), state)


def layer_tensor(layer_index, fibre):
    angle_in = fibre[0]
    angle_out = fibre[1]
    fibre_x = jnp.cos(angle_in) * jnp.cos(angle_out)
    fibre_y = jnp.sin(angle_in) * jnp.cos(angle_out)
    fibre_z = jnp.sin(angle_out)
    spread = longitudinal - transverse
    tensor_table = jnp.stack(
        [
            transverse + spread * fibre_x * fibre_x,
            transverse + spread * fibre_y * fibre_y,
            transverse + spread * fibre_z * fibre_z,
            spread * fibre_x * fibre_y,
            spread * fibre_x * fibre_z,
            spread * fibre_y * fibre_z,
        ]
    )
    layer_ids = jnp.arange(fibre.shape[1], dtype=jnp.int32)
    chosen = layer_index[:, None] == layer_ids[None, :]
    return jnp.sum(jnp.where(chosen[None], tensor_table[:, None, :], jnp.float32(0.0)), axis=2)


def weights(tensor, offset_x, offset_y, offset_z):
    if offset_z == 0:
        if offset_x != 0 and offset_y != 0:
            return offset_x * offset_y * tensor[3] / 2.0
        if offset_x != 0:
            return tensor[0]
        return tensor[1]
    extent_z = tensor.shape[1]
    padded_tensor = jnp.pad(tensor, ((0, 0), (1, 1)), mode="edge")
    averaged = (tensor + padded_tensor[:, 1 + offset_z : 1 + offset_z + extent_z]) / 2.0
    if offset_x == 0 and offset_y == 0:
        return averaged[2]
    if offset_x != 0:
        return offset_x * offset_z * averaged[4] / 2.0
    return offset_y * offset_z * averaged[5] / 2.0


def stencil(volt_shell, mask_shell, tensor):
    volt_padded = jnp.pad(volt_shell, ((0, 0), (1, 1), (0, 0)))
    mask_padded = jnp.pad(mask_shell, ((0, 0), (1, 1), (0, 0)))
    extent_x = volt_shell.shape[0] - 2
    extent_z = volt_shell.shape[1]
    extent_y = volt_shell.shape[2] - 2
    centre = volt_padded[1 : 1 + extent_x, 1 : 1 + extent_z, 1 : 1 + extent_y]
    mask_centre = mask_padded[1 : 1 + extent_x, 1 : 1 + extent_z, 1 : 1 + extent_y]
    flux_sum = jnp.zeros_like(centre)
    for offset_x in (-1, 0, 1):
        for offset_y in (-1, 0, 1):
            for offset_z in (-1, 0, 1):
                length = offset_x * offset_x + offset_y * offset_y + offset_z * offset_z
                if length == 0 or length > 2:
                    continue
                weight = weights(tensor, offset_x, offset_y, offset_z)[None, :, None]
                neighbour = volt_padded[
                    1 + offset_x : 1 + offset_x + extent_x,
                    1 + offset_z : 1 + offset_z + extent_z,
                    1 + offset_y : 1 + offset_y + extent_y,
                ]
                mask_near = mask_padded[
                    1 + offset_x : 1 + offset_x + extent_x,
                    1 + offset_z : 1 + offset_z + extent_z,
                    1 + offset_y : 1 + offset_y + extent_y,
                ]
                flux_sum = flux_sum + weight * mask_near * (neighbour - centre)
    return mask_centre * flux_sum


def double_steps(state, wide_inside, wide_float, inner_inside, inner_float, tensor, widen):
    for repeat in range(STEPS // 2):
        extended = widen(state)
        first = advance(extended, wide_inside)
        middle = first[:, 1:-1, :, 1:-1]
        middle = middle.at[0].set(middle[0] + stencil(first[0], wide_float, tensor))
        second = advance(middle, inner_inside)
        final_volt = second[0][1:-1, :, 1:-1] + stencil(second[0], inner_float, tensor)
        state = second[:, 1:-1, :, 1:-1].at[0].set(final_volt)
    return state


def shards(state, tissue_mask, layer_index, fibre):
    tensor = layer_tensor(layer_index, fibre)
    cells_x, extent_z, block_count = tissue_mask.shape
    spread = jnp.broadcast_to(
        tissue_mask[:, :, :, None], (cells_x, extent_z, block_count, MASK_BLOCK)
    )
    voxel_mask = spread.reshape(cells_x, extent_z, block_count * MASK_BLOCK)
    shelled = padded(voxel_mask, (("gx", 0), ("gy", 2)), 2)
    wide_inside = shelled > 0
    wide_float = wide_inside.astype(jnp.float32)
    inner_inside = wide_inside[1:-1, :, 1:-1]
    inner_float = wide_float[1:-1, :, 1:-1]

    def widen_whole(current):
        return padded(current, (("gx", 1), ("gy", 3)), 2)

    state = double_steps(
        state, wide_inside, wide_float, inner_inside, inner_float, tensor, widen_whole
    )
    return state


def solution(mesh):
    placed = (P(None, "gx", None, "gy"), P("gx", None, "gy"), P(), P())
    return jax.shard_map(
        shards, mesh=mesh, in_specs=placed, out_specs=P(None, "gx", None, "gy"), check_vma=False
    )
```

profile of v0, /device:TPU:91, one launch (start us, length us, event | category | flops | bytes accessed | tf_op | source)
XLA Modules:
  0.0 263.5 jit_solution(3571473226060023119)
XLA Ops:
  0.9 6.3 %collective-permute-start = (s32[2,16,256]{2,1,0:T(8,128)S(1)}, s32[2,16,256]{2,1,0:T(8,128)S(1)}, u32[]{:S(2)}, u32[]{:S(2)}) collective-permute-start(s32[2,16,256]{2,1,0:T(8,128)S(1)} %slice.1836), channel_id=1, source_target_pairs={{0,8},{8,16},{16,24},{24,32},{32,40},{40,48},{48,56},{56,64},{64,7... | collective-permute-start | bytes 98312 | tf_op jit(solution)/shard_map/ppermute | solution.py:30
  13.3 7.9 %collective-permute-start.4 = (f32[12,2,16,256]{3,2,1,0:T(8,128)S(1)}, f32[12,2,16,256]{3,2,1,0:T(8,128)}, u32[]{:S(2)}, u32[]{:S(2)}) collective-permute-start(f32[12,2,16,256]{3,2,1,0:T(8,128)S(1)} %get-tuple-element.130), channel_id=1, source_target_pairs={{0,8},{8,16},{16,24},{24,32},{32,40},{40,48},{48,56},{56,64},{64,7... | collective-permute-start | bytes 1179656 | tf_op jit(solution)/shard_map/ppermute | solution.py:30
  26.9 3.5 %collective-permute-start.3 = (s32[12,16,2]{2,1,0:T(8,128)S(1)}, s32[12,16,2]{2,1,0:T(8,128)}, u32[]{:S(2)}, u32[]{:S(2)}) collective-permute-start(s32[12,16,2]{2,1,0:T(8,128)S(1)} %get-tuple-element.132), channel_id=1, source_target_pairs={{1,0},{2,1},{3,2},{4,3},{5,4},{6,5},{7,6},{9,8},{10,9},{11,10},{12... | collective-permute-start | bytes 4616 | tf_op jit(solution)/shard_map/ppermute | solution.py:31
  36.4 2.8 %copy.50 = f32[12,12,16,2]{2,3,1,0:T(2,128)} copy(f32[12,12,16,2]{3,2,1,0:T(8,128)} %get-tuple-element.121) | data formatting | bytes 36864
  43.4 3.7 %collective-permute-start.6 = (f32[12,12,16,2]{2,3,1,0:T(2,128)}, f32[12,12,16,2]{2,3,1,0:T(2,128)}, u32[]{:S(2)}, u32[]{:S(2)}) collective-permute-start(f32[12,12,16,2]{2,3,1,0:T(2,128)} %copy.50), channel_id=1, source_target_pairs={{0,1},{1,2},{2,3},{3,4},{4,5},{5,6},{6,7},{8,9},{9,10},{10,11},{11... | collective-permute-start | bytes 55304 | tf_op jit(solution)/shard_map/ppermute | solution.py:30
  50.5 2.9 %copy.36 = f32[12,12,16,2]{3,2,1,0:T(8,128)} copy(f32[12,12,16,2]{2,3,1,0:T(2,128)} %collective-permute-done.6) | data formatting | bytes 36864 | tf_op jit(solution)/shard_map/ppermute | solution.py:30
  53.4 2.8 %copy.37 = f32[12,12,16,2]{3,2,1,0:T(8,128)} copy(f32[12,12,16,2]{2,3,1,0:T(2,128)} %collective-permute-done.7) | data formatting | bytes 36864 | tf_op jit(solution)/shard_map/ppermute | solution.py:31
  56.2 2.9 %pad_maximum_fusion = f32[12,12,16,260]{3,2,1,0:T(8,128)S(1)} fusion(f32[12,12,16,2]{3,2,1,0:T(8,128)} %copy.37, f32[12,12,16,256]{3,2,1,0:T(8,128)S(1)} %constant_dynamic-update-slice_fusion.3, f32[12,12,16,2]{3,2,1,0:T(8,128)} %copy.36), kind=kLoop, calls=%fused_computation | loop fusion | flops 1198080 | bytes 4792320 | tf_op jit(solution)/shard_map/concatenate | solution.py:32
  76.2 9.9 %collective-permute-start.8 = (f32[12,2,16,256]{3,2,1,0:T(8,128)S(1)}, f32[12,2,16,256]{3,2,1,0:T(8,128)S(1)}, u32[]{:S(2)}, u32[]{:S(2)}) collective-permute-start(f32[12,2,16,256]{3,2,1,0:T(8,128)S(1)} %get-tuple-element.127), channel_id=1, source_target_pairs={{0,8},{8,16},{16,24},{24,32},{32,40},{40,48},{48,56},{56,64},{64,7... | collective-permute-start | bytes 1179656 | tf_op jit(solution)/shard_map/ppermute | solution.py:30
  88.0 4.5 %collective-permute-done.8 = f32[12,2,16,256]{3,2,1,0:T(8,128)S(1)} collective-permute-done((f32[12,2,16,256]{3,2,1,0:T(8,128)S(1)}, f32[12,2,16,256]{3,2,1,0:T(8,128)S(1)}, u32[]{:S(2)}, u32[]{:S(2)}) %collective-permute-start.8) | collective-permute-done | bytes 393248 | tf_op jit(solution)/shard_map/ppermute | solution.py:30
  92.5 8.1 %collective-permute-done.9 = f32[12,2,16,256]{3,2,1,0:T(8,128)S(1)} collective-permute-done((f32[12,2,16,256]{3,2,1,0:T(8,128)S(1)}, f32[12,2,16,256]{3,2,1,0:T(8,128)S(1)}, u32[]{:S(2)}, u32[]{:S(2)}) %collective-permute-start.9) | collective-permute-done | bytes 393248 | tf_op jit(solution)/shard_map/ppermute | solution.py:31
  103.1 2.8 %copy.52 = f32[12,12,16,2]{2,3,1,0:T(2,128)} copy(f32[12,12,16,2]{3,2,1,0:T(8,128)} %get-tuple-element.119) | data formatting | bytes 36864
  105.9 8.2 %collective-permute-start.10 = (f32[12,12,16,2]{2,3,1,0:T(2,128)}, f32[12,12,16,2]{2,3,1,0:T(2,128)}, u32[]{:S(2)}, u32[]{:S(2)}) collective-permute-start(f32[12,12,16,2]{2,3,1,0:T(2,128)} %copy.52), channel_id=1, source_target_pairs={{0,1},{1,2},{2,3},{3,4},{4,5},{5,6},{6,7},{8,9},{9,10},{10,11},{11... | collective-permute-start | bytes 55304 | tf_op jit(solution)/shard_map/ppermute | solution.py:30
  121.9 2.8 %copy.41 = f32[12,12,16,2]{3,2,1,0:T(8,128)} copy(f32[12,12,16,2]{2,3,1,0:T(2,128)} %collective-permute-done.11) | data formatting | bytes 36864 | tf_op jit(solution)/shard_map/ppermute | solution.py:31
  144.3 3.2 %collective-permute-start.12 = (f32[12,2,16,256]{3,2,1,0:T(8,128)S(1)}, f32[12,2,16,256]{3,2,1,0:T(8,128)S(1)}, u32[]{:S(2)}, u32[]{:S(2)}) collective-permute-start(f32[12,2,16,256]{3,2,1,0:T(8,128)S(1)} %get-tuple-element.125), channel_id=1, source_target_pairs={{0,8},{8,16},{16,24},{24,32},{32,40},{40,48},{48,56},{56,64},{64,7... | collective-permute-start | bytes 1179656 | tf_op jit(solution)/shard_map/ppermute | solution.py:30
  152.2 12.9 %collective-permute-done.13 = f32[12,2,16,256]{3,2,1,0:T(8,128)S(1)} collective-permute-done((f32[12,2,16,256]{3,2,1,0:T(8,128)S(1)}, f32[12,2,16,256]{3,2,1,0:T(8,128)S(1)}, u32[]{:S(2)}, u32[]{:S(2)}) %collective-permute-start.13) | collective-permute-done | bytes 393248 | tf_op jit(solution)/shard_map/ppermute | solution.py:31
  167.5 2.8 %copy.54 = f32[12,12,16,2]{2,3,1,0:T(2,128)} copy(f32[12,12,16,2]{3,2,1,0:T(8,128)} %get-tuple-element.117) | data formatting | bytes 36864
  173.8 4.7 %collective-permute-start.15 = (f32[12,12,16,2]{2,3,1,0:T(2,128)}, f32[12,12,16,2]{2,3,1,0:T(2,128)}, u32[]{:S(2)}, u32[]{:S(2)}) collective-permute-start(f32[12,12,16,2]{2,3,1,0:T(2,128)} %copy.55), channel_id=1, source_target_pairs={{1,0},{2,1},{3,2},{4,3},{5,4},{6,5},{7,6},{9,8},{10,9},{11,10},{12... | collective-permute-start | bytes 55304 | tf_op jit(solution)/shard_map/ppermute | solution.py:31
  180.8 2.8 %copy.45 = f32[12,12,16,2]{3,2,1,0:T(8,128)} copy(f32[12,12,16,2]{2,3,1,0:T(2,128)} %collective-permute-done.15) | data formatting | bytes 36864 | tf_op jit(solution)/shard_map/ppermute | solution.py:31
  203.2 2.9 %collective-permute-start.16 = (f32[12,2,16,256]{3,2,1,0:T(8,128)S(1)}, f32[12,2,16,256]{3,2,1,0:T(8,128)S(1)}, u32[]{:S(2)}, u32[]{:S(2)}) collective-permute-start(f32[12,2,16,256]{3,2,1,0:T(8,128)S(1)} %get-tuple-element.123), channel_id=1, source_target_pairs={{0,8},{8,16},{16,24},{24,32},{32,40},{40,48},{48,56},{56,64},{64,7... | collective-permute-start | bytes 1179656 | tf_op jit(solution)/shard_map/ppermute | solution.py:30
  210.8 12.9 %collective-permute-done.17 = f32[12,2,16,256]{3,2,1,0:T(8,128)S(1)} collective-permute-done((f32[12,2,16,256]{3,2,1,0:T(8,128)S(1)}, f32[12,2,16,256]{3,2,1,0:T(8,128)S(1)}, u32[]{:S(2)}, u32[]{:S(2)}) %collective-permute-start.17) | collective-permute-done | bytes 393248 | tf_op jit(solution)/shard_map/ppermute | solution.py:31
  226.1 2.8 %copy.56 = f32[12,12,16,2]{2,3,1,0:T(2,128)} copy(f32[12,12,16,2]{3,2,1,0:T(8,128)} %get-tuple-element.115) | data formatting | bytes 36864
  232.4 4.5 %collective-permute-start.19 = (f32[12,12,16,2]{2,3,1,0:T(2,128)}, f32[12,12,16,2]{2,3,1,0:T(2,128)}, u32[]{:S(2)}, u32[]{:S(2)}) collective-permute-start(f32[12,12,16,2]{2,3,1,0:T(2,128)} %copy.57), channel_id=1, source_target_pairs={{1,0},{2,1},{3,2},{4,3},{5,4},{6,5},{7,6},{9,8},{10,9},{11,10},{12... | collective-permute-start | bytes 55304 | tf_op jit(solution)/shard_map/ppermute | solution.py:31
  239.1 2.8 %copy.49 = f32[12,12,16,2]{3,2,1,0:T(8,128)} copy(f32[12,12,16,2]{2,3,1,0:T(2,128)} %collective-permute-done.19) | data formatting | bytes 36864 | tf_op jit(solution)/shard_map/ppermute | solution.py:31
  (239 shorter events, 140.5 us)
Async XLA Ops:
  0.9 23.2 %collective-permute-start = (s32[2,16,256]{2,1,0:T(8,128)S(1)}, s32[2,16,256]{2,1,0:T(8,128)S(1)}, u32[]{:S(2)}, u32[]{:S(2)}) collective-permute-start(s32[2,16,256]{2,1,0:T(8,128)S(1)} %slice.1836), channel_id=1, source_target_pairs={{0,8},{8,16},{16,24},{24,32},{32,40},{40,48},{48,56},{56,64},{64,7... | collective-permute-start | bytes 98312 | tf_op jit(solution)/shard_map/ppermute | solution.py:30
  7.5 16.7 %collective-permute-start.1 = (s32[2,16,256]{2,1,0:T(8,128)S(1)}, s32[2,16,256]{2,1,0:T(8,128)S(1)}, u32[]{:S(2)}, u32[]{:S(2)}) collective-permute-start(s32[2,16,256]{2,1,0:T(8,128)S(1)} %slice.1838), channel_id=1, source_target_pairs={{8,0},{16,8},{24,16},{32,24},{40,32},{48,40},{56,48},{64,56},{72,6... | collective-permute-start | bytes 98312 | tf_op jit(solution)/shard_map/ppermute | solution.py:31
  11.4 23.2 %collective-permute-start.5 = (f32[12,2,16,256]{3,2,1,0:T(8,128)}, f32[12,2,16,256]{3,2,1,0:T(8,128)S(1)}, u32[]{:S(2)}, u32[]{:S(2)}) collective-permute-start(f32[12,2,16,256]{3,2,1,0:T(8,128)} %get-tuple-element.129), channel_id=1, source_target_pairs={{8,0},{16,8},{24,16},{32,24},{40,32},{48,40},{56,48},{64,56},{72,6... | collective-permute-start | bytes 1179656 | tf_op jit(solution)/shard_map/ppermute | solution.py:31
  13.3 18.6 %collective-permute-start.4 = (f32[12,2,16,256]{3,2,1,0:T(8,128)S(1)}, f32[12,2,16,256]{3,2,1,0:T(8,128)}, u32[]{:S(2)}, u32[]{:S(2)}) collective-permute-start(f32[12,2,16,256]{3,2,1,0:T(8,128)S(1)} %get-tuple-element.130), channel_id=1, source_target_pairs={{0,8},{8,16},{16,24},{24,32},{32,40},{40,48},{48,56},{56,64},{64,7... | collective-permute-start | bytes 1179656 | tf_op jit(solution)/shard_map/ppermute | solution.py:30
  24.3 22.8 %collective-permute-start.2 = (s32[12,16,2]{2,1,0:T(8,128)S(1)}, s32[12,16,2]{2,1,0:T(8,128)S(1)}, u32[]{:S(2)}, u32[]{:S(2)}) collective-permute-start(s32[12,16,2]{2,1,0:T(8,128)S(1)} %get-tuple-element.131), channel_id=1, source_target_pairs={{0,1},{1,2},{2,3},{3,4},{4,5},{5,6},{6,7},{8,9},{9,10},{10,11},{11... | collective-permute-start | bytes 4616 | tf_op jit(solution)/shard_map/ppermute | solution.py:30
  26.9 20.1 %collective-permute-start.3 = (s32[12,16,2]{2,1,0:T(8,128)S(1)}, s32[12,16,2]{2,1,0:T(8,128)}, u32[]{:S(2)}, u32[]{:S(2)}) collective-permute-start(s32[12,16,2]{2,1,0:T(8,128)S(1)} %get-tuple-element.132), channel_id=1, source_target_pairs={{1,0},{2,1},{3,2},{4,3},{5,4},{6,5},{7,6},{9,8},{10,9},{11,10},{12... | collective-permute-start | bytes 4616 | tf_op jit(solution)/shard_map/ppermute | solution.py:31
  41.5 11.9 %collective-permute-start.7 = (f32[12,12,16,2]{2,3,1,0:T(2,128)S(1)}, f32[12,12,16,2]{2,3,1,0:T(2,128)}, u32[]{:S(2)}, u32[]{:S(2)}) collective-permute-start(f32[12,12,16,2]{2,3,1,0:T(2,128)S(1)} %copy.51), channel_id=1, source_target_pairs={{1,0},{2,1},{3,2},{4,3},{5,4},{6,5},{7,6},{9,8},{10,9},{11,10},{12... | collective-permute-start | bytes 55304 | tf_op jit(solution)/shard_map/ppermute | solution.py:31
  43.4 7.1 %collective-permute-start.6 = (f32[12,12,16,2]{2,3,1,0:T(2,128)}, f32[12,12,16,2]{2,3,1,0:T(2,128)}, u32[]{:S(2)}, u32[]{:S(2)}) collective-permute-start(f32[12,12,16,2]{2,3,1,0:T(2,128)} %copy.50), channel_id=1, source_target_pairs={{0,1},{1,2},{2,3},{3,4},{4,5},{5,6},{6,7},{8,9},{9,10},{10,11},{11... | collective-permute-start | bytes 55304 | tf_op jit(solution)/shard_map/ppermute | solution.py:30
  76.2 16.3 %collective-permute-start.8 = (f32[12,2,16,256]{3,2,1,0:T(8,128)S(1)}, f32[12,2,16,256]{3,2,1,0:T(8,128)S(1)}, u32[]{:S(2)}, u32[]{:S(2)}) collective-permute-start(f32[12,2,16,256]{3,2,1,0:T(8,128)S(1)} %get-tuple-element.127), channel_id=1, source_target_pairs={{0,8},{8,16},{16,24},{24,32},{32,40},{40,48},{48,56},{56,64},{64,7... | collective-permute-start | bytes 1179656 | tf_op jit(solution)/shard_map/ppermute | solution.py:30
  86.1 14.6 %collective-permute-start.9 = (f32[12,2,16,256]{3,2,1,0:T(8,128)S(1)}, f32[12,2,16,256]{3,2,1,0:T(8,128)S(1)}, u32[]{:S(2)}, u32[]{:S(2)}) collective-permute-start(f32[12,2,16,256]{3,2,1,0:T(8,128)S(1)} %get-tuple-element.128), channel_id=1, source_target_pairs={{8,0},{16,8},{24,16},{32,24},{40,32},{48,40},{56,48},{64,56},{72,6... | collective-permute-start | bytes 1179656 | tf_op jit(solution)/shard_map/ppermute | solution.py:31
  92.5 8.1 %copy-start.7 = (f32[12,2,16,256]{3,2,1,0:T(8,128)}, f32[12,2,16,256]{3,2,1,0:T(8,128)S(1)}, u32[]{:S(2)}) copy-start(f32[12,2,16,256]{3,2,1,0:T(8,128)S(1)} %collective-permute-done.8) | copy-start | bytes 1179652
  105.9 11.9 %collective-permute-start.10 = (f32[12,12,16,2]{2,3,1,0:T(2,128)}, f32[12,12,16,2]{2,3,1,0:T(2,128)}, u32[]{:S(2)}, u32[]{:S(2)}) collective-permute-start(f32[12,12,16,2]{2,3,1,0:T(2,128)} %copy.52), channel_id=1, source_target_pairs={{0,1},{1,2},{2,3},{3,4},{4,5},{5,6},{6,7},{8,9},{9,10},{10,11},{11... | collective-permute-start | bytes 55304 | tf_op jit(solution)/shard_map/ppermute | solution.py:30
  115.7 6.2 %collective-permute-start.11 = (f32[12,12,16,2]{2,3,1,0:T(2,128)}, f32[12,12,16,2]{2,3,1,0:T(2,128)}, u32[]{:S(2)}, u32[]{:S(2)}) collective-permute-start(f32[12,12,16,2]{2,3,1,0:T(2,128)} %copy.53), channel_id=1, source_target_pairs={{1,0},{2,1},{3,2},{4,3},{5,4},{6,5},{7,6},{9,8},{10,9},{11,10},{12... | collective-permute-start | bytes 55304 | tf_op jit(solution)/shard_map/ppermute | solution.py:31
  131.0 2.0 copy-start.2
  144.3 7.9 %collective-permute-start.12 = (f32[12,2,16,256]{3,2,1,0:T(8,128)S(1)}, f32[12,2,16,256]{3,2,1,0:T(8,128)S(1)}, u32[]{:S(2)}, u32[]{:S(2)}) collective-permute-start(f32[12,2,16,256]{3,2,1,0:T(8,128)S(1)} %get-tuple-element.125), channel_id=1, source_target_pairs={{0,8},{8,16},{16,24},{24,32},{32,40},{40,48},{48,56},{56,64},{64,7... | collective-permute-start | bytes 1179656 | tf_op jit(solution)/shard_map/ppermute | solution.py:30
  147.4 17.6 %collective-permute-start.13 = (f32[12,2,16,256]{3,2,1,0:T(8,128)S(1)}, f32[12,2,16,256]{3,2,1,0:T(8,128)S(1)}, u32[]{:S(2)}, u32[]{:S(2)}) collective-permute-start(f32[12,2,16,256]{3,2,1,0:T(8,128)S(1)} %get-tuple-element.126), channel_id=1, source_target_pairs={{8,0},{16,8},{24,16},{32,24},{40,32},{48,40},{56,48},{64,56},{72,6... | collective-permute-start | bytes 1179656 | tf_op jit(solution)/shard_map/ppermute | solution.py:31
  152.2 12.9 %copy-start.9 = (f32[12,2,16,256]{3,2,1,0:T(8,128)}, f32[12,2,16,256]{3,2,1,0:T(8,128)S(1)}, u32[]{:S(2)}) copy-start(f32[12,2,16,256]{3,2,1,0:T(8,128)S(1)} %collective-permute-done.12) | copy-start | bytes 1179652
  170.3 8.2 %collective-permute-start.14 = (f32[12,12,16,2]{2,3,1,0:T(2,128)}, f32[12,12,16,2]{2,3,1,0:T(2,128)}, u32[]{:S(2)}, u32[]{:S(2)}) collective-permute-start(f32[12,12,16,2]{2,3,1,0:T(2,128)} %copy.54), channel_id=1, source_target_pairs={{0,1},{1,2},{2,3},{3,4},{4,5},{5,6},{6,7},{8,9},{9,10},{10,11},{11... | collective-permute-start | bytes 55304 | tf_op jit(solution)/shard_map/ppermute | solution.py:30
  173.8 7.0 %collective-permute-start.15 = (f32[12,12,16,2]{2,3,1,0:T(2,128)}, f32[12,12,16,2]{2,3,1,0:T(2,128)}, u32[]{:S(2)}, u32[]{:S(2)}) collective-permute-start(f32[12,12,16,2]{2,3,1,0:T(2,128)} %copy.55), channel_id=1, source_target_pairs={{1,0},{2,1},{3,2},{4,3},{5,4},{6,5},{7,6},{9,8},{10,9},{11,10},{12... | collective-permute-start | bytes 55304 | tf_op jit(solution)/shard_map/ppermute | solution.py:31
  203.2 7.6 %collective-permute-start.16 = (f32[12,2,16,256]{3,2,1,0:T(8,128)S(1)}, f32[12,2,16,256]{3,2,1,0:T(8,128)S(1)}, u32[]{:S(2)}, u32[]{:S(2)}) collective-permute-start(f32[12,2,16,256]{3,2,1,0:T(8,128)S(1)} %get-tuple-element.123), channel_id=1, source_target_pairs={{0,8},{8,16},{16,24},{24,32},{32,40},{40,48},{48,56},{56,64},{64,7... | collective-permute-start | bytes 1179656 | tf_op jit(solution)/shard_map/ppermute | solution.py:30
  206.1 17.6 %collective-permute-start.17 = (f32[12,2,16,256]{3,2,1,0:T(8,128)S(1)}, f32[12,2,16,256]{3,2,1,0:T(8,128)S(1)}, u32[]{:S(2)}, u32[]{:S(2)}) collective-permute-start(f32[12,2,16,256]{3,2,1,0:T(8,128)S(1)} %get-tuple-element.124), channel_id=1, source_target_pairs={{8,0},{16,8},{24,16},{32,24},{40,32},{48,40},{56,48},{64,56},{72,6... | collective-permute-start | bytes 1179656 | tf_op jit(solution)/shard_map/ppermute | solution.py:31
  210.8 12.9 %copy-start.5 = (f32[12,2,16,256]{3,2,1,0:T(8,128)}, f32[12,2,16,256]{3,2,1,0:T(8,128)S(1)}, u32[]{:S(2)}) copy-start(f32[12,2,16,256]{3,2,1,0:T(8,128)S(1)} %collective-permute-done.16) | copy-start | bytes 1179652
  228.9 8.0 %collective-permute-start.18 = (f32[12,12,16,2]{2,3,1,0:T(2,128)}, f32[12,12,16,2]{2,3,1,0:T(2,128)}, u32[]{:S(2)}, u32[]{:S(2)}) collective-permute-start(f32[12,12,16,2]{2,3,1,0:T(2,128)} %copy.56), channel_id=1, source_target_pairs={{0,1},{1,2},{2,3},{3,4},{4,5},{5,6},{6,7},{8,9},{9,10},{10,11},{11... | collective-permute-start | bytes 55304 | tf_op jit(solution)/shard_map/ppermute | solution.py:30
  232.4 6.7 %collective-permute-start.19 = (f32[12,12,16,2]{2,3,1,0:T(2,128)}, f32[12,12,16,2]{2,3,1,0:T(2,128)}, u32[]{:S(2)}, u32[]{:S(2)}) collective-permute-start(f32[12,12,16,2]{2,3,1,0:T(2,128)} %copy.57), channel_id=1, source_target_pairs={{1,0},{2,1},{3,2},{4,3},{5,4},{6,5},{7,6},{9,8},{10,9},{11,10},{12... | collective-permute-start | bytes 55304 | tf_op jit(solution)/shard_map/ppermute | solution.py:31
  (13 other events, 22.4 us)
where the time goes:
time: 268 us; the launch traced here: 263 us
  other arithmetic  76.3 us (28%)
  starting transfers between devices  74.7 us (28%)
  local copies, waits for them, and re-layouts  60.3 us (22%)
  waiting for transfers between devices  50.7 us (19%)
    ppermute x10, starting transfers between devices, padded(): before = lax.ppermute(last, axis, up)  48.4 us
    unnamed x88, other arithmetic  37.8 us
    ppermute x10, waiting for transfers between devices, padded(): after = lax.ppermute(leading, axis, down)  37.1 us
    ppermute x10, starting transfers between devices, padded(): after = lax.ppermute(leading, axis, down)  26.2 us
    unnamed x47, local copies, waits for them, and re-layouts  24.1 us
    ppermute x10, waiting for transfers between devices, padded(): before = lax.ppermute(last, axis, up)  13.7 us
    concatenate x7, other arithmetic, padded(): x = jnp.concatenate([before, x, after], axis=dim)  11.8 us
    ppermute x4, local copies, waits for them, and re-layouts, padded(): after = lax.ppermute(leading, axis, down)  11.3 us
  transfers between devices with their start and end apart: 20, of which 11 were waited for; matrix products, arithmetic and copies ran while one was open for 11% of the time, Pallas kernels for 0%

commit v1 on v0

v1 whole, which is shorter than its diff:
```python
import math

import jax
import jax.numpy as jnp
from jax import lax
from jax.experimental import pallas as pl
from jax.experimental.pallas import tpu as pltpu
from jax.sharding import PartitionSpec as P

STEPS = 8
TRANSVERSE = 0.04
LONGITUDINAL = 0.12
DT = 0.02
RTF = 8314.472 * 310.0 / 96485.3415
EK = RTF * math.log(5.4 / 138.3)
ENA = RTF * math.log(140.0 / 7.67)
EKS = RTF * math.log((5.4 + 0.03 * 140.0) / (138.3 + 0.03 * 7.67))
L2E = 1.0 / math.log(2.0)
KAPPA = -DT * L2E


def grow(volt, slope):
    return jnp.exp2(volt * (slope * L2E))


def sig(volt, centre, width):
    return jax.nn.sigmoid(volt * (1.0 / width) + (-centre / width))


def settle(gate, steady, factor):
    return steady + (gate - steady) * jnp.exp2(factor)


def membrane(s):
    x, m, h, j, d, f, r, z, p, q, w, ca = s
    v = x * 100.0
    over = v - EK
    b = grow(v, 0.05)
    ib = 1.0 / b
    b2 = b * b
    ib2 = ib * ib
    c = jnp.maximum(ca, 0.02)
    vca = (v - 0.5 * RTF * math.log(2000.0)) + (0.5 * RTF) * jnp.log(c)
    sodium = ((14.838 * m) * (m * m) * (h * j) + 0.00029) * (v - ENA)
    calcium = (0.08 * d * f + 0.000592) * vca
    sa = sig(v, EK + 200.0, -1.0 / 0.06)
    bk = (
        (30.0 * math.exp(0.0002 * (100.0 - EK))) * grow(v, 0.0002)
        + (10.0 * math.exp(0.1 * (-EK - 10.0))) * b2
    ) * sig(v, EK, 2.0)
    inward = 5.405 * sa / (sa + bk)
    potassium = (
        0.294 * r * z + 0.153 * p * q + inward + 0.0146 * sig(v, 25.0, 5.98)
    ) * over
    slow = (0.392 * w) * w * (v - EKS)
    en = grow(v, -1.0 / RTF)
    pump = (2.724 * 5.4 / 6.4 * 7.67 / 47.67) / (
        1.0 + 0.1245 * grow(v, -0.1 / RTF) + 0.0353 * en
    )
    ef = grow(v, 0.35 / RTF)
    eg = ef * en
    scale = 1000.0 / ((87.5**3 + 140.0**3) * 3.38)
    exchange = (
        (scale * 7.67**3 * 2.0) * ef - (scale * 2.5 * 140.0**3 * 0.001) * eg * c
    ) / (1.0 + 0.1 * eg)
    pump_ca = 0.1238 * c / (c + 0.5)
    total = sodium + calcium + potassium + slow + pump + exchange + pump_ca
    nx = x - (DT / 100.0) * total
    nca = ca - (DT * 0.05) * (calcium + pump_ca - 2.0 * exchange)
    low = 1.0 / (1.0 + math.exp(20.0) * grow(v, 0.5))
    nm = settle(
        m,
        sig(v, -56.86, 9.03) ** 2,
        (10.0 * KAPPA + (10.0 * KAPPA * math.exp(-12.0)) * (ib2 * ib2))
        / (sig(v, -35.0, -5.0) + sig(v, 50.0, -200.0)),
    )
    hs = sig(v, -71.55, -7.43)
    hs = hs * hs
    up = (KAPPA * 0.77 / 0.13) * sig(v, -10.66, 11.1)
    dn = (
        (KAPPA * 0.057 * math.exp(-80.0 / 6.8)) * grow(v, -1.0 / 6.8)
        + (KAPPA * 2.7) * grow(v, 0.079)
        + (KAPPA * 310000.0) * grow(v, 0.3485)
    )
    nh = settle(h, hs, up + low * (dn - up))
    up = (KAPPA * 0.6) * grow(v, 0.057) * sig(v, -32.0, 10.0)
    dn = ((KAPPA * -25428.0) * grow(v, 0.2444) - (KAPPA * 6.948e-06) * grow(v, -0.04391)) * (
        v + 37.78
    ) * sig(v, -79.23, -1.0 / 0.311) + (KAPPA * 0.02424) * grow(v, -0.01052) * sig(
        v, -40.14, 1.0 / 0.1378
    )
    nj = settle(j, hs, up + low * (dn - up))
    nd = settle(
        d,
        sig(v, -8.0, 7.5),
        KAPPA
        / ((1.96 * sig(v, -35.0, 13.0) + 0.35) * sig(v, -5.0, -5.0) + sig(v, 50.0, 20.0)),
    )
    t = v + 27.0
    nf = settle(
        f,
        sig(v, -20.0, -7.0),
        1.0
        / (
            (1102.5 / KAPPA) * jnp.exp2(t * t * (-L2E / 225.0))
            + (200.0 / KAPPA) * sig(v, 13.0, 10.0)
            + (180.0 / KAPPA) * sig(v, -30.0, -10.0)
            + 20.0 / KAPPA
        ),
    )
    t = v + 40.0
    nr = settle(
        r,
        sig(v, 20.0, 6.0),
        1.0 / ((9.5 / KAPPA) * jnp.exp2(t * t * (-L2E / 1800.0)) + 0.8 / KAPPA),
    )
    t = v + 45.0
    nz = settle(
        z,
        sig(v, -20.0, -5.0),
        1.0
        / (
            (85.0 / KAPPA) * jnp.exp2(t * t * (-L2E / 320.0))
            + (5.0 / KAPPA) * sig(v, 20.0, -5.0)
            + 3.0 / KAPPA
        ),
    )
    k = KAPPA / 2700.0
    np_ = settle(
        p,
        sig(v, -26.0, 7.0),
        (k + (k * math.exp(-4.5)) * ib2)
        * (1.0 + math.exp(30.0 / 11.5) * grow(v, 1.0 / 11.5)),
    )
    k = KAPPA / 3.36
    nq = settle(
        q,
        sig(v, -88.0, -24.0),
        (k * (1.0 + math.exp(-6.0))) + (k * math.exp(-3.0)) * (b + ib),
    )
    nw = settle(
        w,
        sig(v, -5.0, 14.0),
        1.0
        / (
            lax.rsqrt(1.0 + math.exp(5.0 / 6.0) * grow(v, -1.0 / 6.0))
            * ((1400.0 / KAPPA) * sig(v, 35.0, -15.0))
            + 80.0 / KAPPA
        ),
    )
    return nx, nm, nh, nj, nd, nf, nr, nz, np_, nq, nw, nca


INNER = 8
COMPS = 12
HOPS = STEPS - 1
MESH = pl.DeviceIdType.MESH


def react(state, inside):
    fresh = membrane(state)
    return [jnp.where(inside, new, old) for new, old in zip(fresh, state)]


def lanes():
    return lax.broadcasted_iota(jnp.int32, (16, 128), 1)


def turn(tile, shift):
    shift = shift % 128
    return tile if shift == 0 else pltpu.roll(tile, shift, 1)


def coefficients(layer_ref, fibre_ref, coef):
    row = lax.broadcasted_iota(jnp.int32, (16, 128), 0)
    angle_in = jnp.zeros((16, 128), jnp.float32)
    angle_out = jnp.zeros((16, 128), jnp.float32)
    for level in range(16):
        layer = layer_ref[level]
        angle_in = jnp.where(row == level, fibre_ref[0, layer], angle_in)
        angle_out = jnp.where(row == level, fibre_ref[1, layer], angle_out)
    along_x = jnp.cos(angle_in) * jnp.cos(angle_out)
    along_y = jnp.sin(angle_in) * jnp.cos(angle_out)
    along_z = jnp.sin(angle_out)
    spread = LONGITUDINAL - TRANSVERSE
    coef[0] = TRANSVERSE + spread * along_x * along_x
    coef[1] = TRANSVERSE + spread * along_y * along_y
    coef[2] = spread * along_x * along_y / 2.0
    parts = (
        TRANSVERSE + spread * along_z * along_z,
        spread * along_x * along_z / 2.0,
        spread * along_y * along_z / 2.0,
    )
    for index, part in enumerate(parts):
        below = (part + pltpu.roll(part, 1, 0)) / 2.0
        above = (part + pltpu.roll(part, 15, 0)) / 2.0
        coef[3 + index] = jnp.where(row == 0, 0.0, below)
        coef[6 + index] = jnp.where(row == 15, 0.0, above)


def tile_sum(coef, here, up, down):
    value, both, slope = here
    across = up[0] - down[0]
    rising = coef[3] * value + coef[4] * across + coef[5] * slope
    falling = coef[6] * value - coef[7] * across - coef[8] * slope
    flat = coef[0] * (up[0] + down[0]) + coef[1] * both + coef[2] * (up[2] - down[2])
    return flat + pltpu.roll(rising, 15, 0) + pltpu.roll(falling, 1, 0)


def plane_shifts(first, second, strip, base):
    lane = lanes()
    right_first, right_second = pltpu.roll(first, 1, 1), pltpu.roll(second, 1, 1)
    left_first, left_second = pltpu.roll(first, 127, 1), pltpu.roll(second, 127, 1)
    before = jnp.where(lane == 0, turn(strip, -(base + 7)), right_first)
    middle_before = jnp.where(lane == 0, right_first, right_second)
    after = jnp.where(lane == 127, turn(strip, 127 - (base + 8)), left_second)
    middle_after = jnp.where(lane == 127, left_second, left_first)
    return (
        (first, middle_after + before, middle_after - before),
        (second, after + middle_before, after - middle_before),
    )


def strip_shifts(strip, edges):
    lane = lanes()
    after, before = pltpu.roll(strip, 127, 1), pltpu.roll(strip, 1, 1)
    for base, first, second in edges:
        after = jnp.where(lane == base + 7, turn(first, base + 7), after)
        before = jnp.where(lane == base + 8, turn(second, base + 9), before)
    return strip, after + before, after - before


def kernel(
    state_ref,
    mask_ref,
    layer_ref,
    fibre_ref,
    out_ref,
    cells,
    packed,
    keep,
    mask,
    strip_cells,
    strip_packed,
    strip_keep,
    strip_mask,
    coef,
    hop_out,
    hop_in,
    first_out,
    first_in,
    gates_out,
    side_out,
    side_in,
    relay_out,
    relay_in,
    relay_gates_out,
    relay_gates_in,
    hop_send,
    hop_recv,
    first_send,
    first_recv,
    gates_send,
    gates_recv,
    side_send,
    side_recv,
    relay_send,
    relay_recv,
    load_sem,
    store_sem,
):
    me_x, me_y = lax.axis_index("gx"), lax.axis_index("gy")
    size_x, size_y = lax.axis_size("gx"), lax.axis_size("gy")
    above = lax.rem(me_x + 1, size_x)
    below = lax.rem(me_x + size_x - 1, size_x)
    right = lax.rem(me_y + 1, size_y)
    left = lax.rem(me_y + size_y - 1, size_y)
    along_x = ((above, me_y), (below, me_y))
    along_y = ((me_x, right), (me_x, left))

    barrier = pltpu.get_barrier_semaphore()
    for target in along_x + along_y:
        pl.semaphore_signal(barrier, inc=1, device_id=target, device_id_type=MESH)

    def remote(source, target, sends, recvs, device):
        return pltpu.make_async_remote_copy(
            src_ref=source,
            dst_ref=target,
            send_sem=sends,
            recv_sem=recvs,
            device_id=device,
            device_id_type=MESH,
        )

    loads = [
        pltpu.make_async_copy(state_ref.at[:, plane], cells.at[:, plane + 1], load_sem.at[plane])
        for plane in range(INNER)
    ]
    for plane in (0, 7, 1, 6, 2, 5, 3, 4):
        loads[plane].start()

    lane = lanes()
    coefficients(layer_ref, fibre_ref, coef)
    spread_tile = jnp.zeros((16, 128), jnp.float32)
    for plane in range(INNER):
        blocks = (mask_ref[plane] > 0).astype(jnp.float32)
        for half in range(2):
            tile = jnp.broadcast_to(blocks[:, half : half + 1], (16, 128))
            mask[plane + 2, :, half * 128 : half * 128 + 128] = tile
            spread_tile = jnp.where(lane == 2 * plane + half, tile, spread_tile)

    def react_plane(slot, parity):
        for top in (0, 8):
            rows = pl.ds(top, 8)
            inside = mask[slot + 1, rows] > 0.0
            fresh = react([cells[comp, slot, rows] for comp in range(COMPS)], inside)
            for comp in range(COMPS):
                cells[comp, slot, rows] = fresh[comp]
            packed[parity, slot + 1, rows] = jnp.where(inside, fresh[0], 0.0)

    def react_strip(which, parity):
        for top in (0, 8):
            rows = pl.ds(top, 8)
            inside = strip_mask[which, rows] > 0.0
            fresh = react([strip_cells[which, comp, rows] for comp in range(COMPS)], inside)
            for comp in range(COMPS):
                strip_cells[which, comp, rows] = fresh[comp]
            strip_packed[parity, which, rows] = jnp.where(inside, fresh[0], 0.0)

    def react_pair(pair, carry, parity):
        react_plane(pair + 1, parity)
        react_plane(8 - pair, parity)
        return carry

    for pair in range(4):
        loads[pair].wait()
        loads[7 - pair].wait()

    lax.fori_loop(0, 4, lambda pair, carry: react_pair(pair, carry, 0), 0)

    for way, (edge, inward) in enumerate(((7, 6), (0, 1))):
        first_out[way, :, 0:256] = packed[0, inward + 2]
        first_out[way, :, 256:512] = cells[0, edge + 1]
        first_out[way, :, 512:640] = spread_tile
        gates_out[way] = cells[1:12, edge + 1]

    def pack_side(read):
        tile = jnp.zeros((16, 128), jnp.float32)
        for plane in range(INNER):
            first, second = read(plane)
            base = plane * 16
            tile = jnp.where((lane >= base) & (lane < base + 8), turn(second, base + 8), tile)
            tile = jnp.where((lane >= base + 8) & (lane < base + 16), turn(first, base + 8), tile)
        return tile

    def own(comp):
        return lambda plane: (cells[comp, plane + 1, :, 0:128], cells[comp, plane + 1, :, 128:256])

    side_out[0] = pack_side(own(0))
    side_out[1] = pack_side(lambda plane: (mask[plane + 2, :, 0:128], mask[plane + 2, :, 128:256]))
    for comp in range(1, COMPS):
        side_out[comp + 1] = pack_side(own(comp))

    pl.semaphore_wait(barrier, 4)
    early, late, lead, bulk, pass_on, pass_gates = [], [], [], [], [], []
    for way in range(2):
        early.append(
            remote(
                side_out.at[pl.ds(0, 2)],
                side_in.at[way, pl.ds(0, 2)],
                side_send.at[0, way],
                side_recv.at[0, way],
                along_y[way],
            )
        )
        lead.append(
            remote(
                first_out.at[way],
                first_in.at[way],
                first_send.at[way],
                first_recv.at[way],
                along_x[way],
            )
        )
        late.append(
            remote(
                side_out.at[pl.ds(2, 11)],
                side_in.at[way, pl.ds(2, 11)],
                side_send.at[1, way],
                side_recv.at[1, way],
                along_y[way],
            )
        )
        bulk.append(
            remote(
                gates_out.at[way],
                cells.at[pl.ds(1, 11), 0 if way == 0 else 9],
                gates_send.at[way],
                gates_recv.at[way],
                along_x[way],
            )
        )
        pass_on.append(
            remote(
                relay_out.at[way],
                relay_in.at[way],
                relay_send.at[0, way],
                relay_recv.at[0, way],
                along_x[way],
            )
        )
        pass_gates.append(
            remote(
                relay_gates_out.at[way],
                relay_gates_in.at[way],
                relay_send.at[1, way],
                relay_recv.at[1, way],
                along_x[way],
            )
        )
    for copies in (early, lead, late, bulk):
        for copy in copies:
            copy.start()

    from_left = lax.rem(lane, 16) < 8
    for copy in early:
        copy.wait_recv()
    strip_cells[0, 0] = jnp.where(from_left, side_in[0, 0], side_in[1, 0])
    reach_left = jnp.where(me_y > 0, 1.0, 0.0)
    reach_right = jnp.where(me_y < size_y - 1, 1.0, 0.0)
    strip_mask[0] = jnp.where(from_left, side_in[0, 1] * reach_left, side_in[1, 1] * reach_right)
    strip_packed[0, 0] = strip_mask[0] * strip_cells[0, 0]
    for way, (edge, inward) in enumerate(((7, 6), (0, 1))):
        tile = jnp.zeros((16, 128), jnp.float32)
        parts = (
            (strip_cells[0, 0], edge),
            (strip_mask[0], edge),
            (strip_mask[0], inward),
            (strip_packed[0, 0], inward),
        )
        for group, (part, plane) in enumerate(parts):
            here = (lane >= group * 16) & (lane < group * 16 + 16)
            tile = jnp.where(here, turn(part, group * 16 - plane * 16), tile)
        relay_out[way] = tile
        pass_on[way].start()

    for copy in late:
        copy.wait_recv()
    for comp in range(1, COMPS):
        strip_cells[0, comp] = jnp.where(from_left, side_in[0, comp + 1], side_in[1, comp + 1])
    for way, edge in enumerate((7, 0)):
        for half, gates in enumerate((range(1, 9), range(9, 12))):
            tile = jnp.zeros((16, 128), jnp.float32)
            for group, comp in enumerate(gates):
                here = (lane >= group * 16) & (lane < group * 16 + 16)
                tile = jnp.where(here, turn(strip_cells[0, comp], group * 16 - edge * 16), tile)
            relay_gates_out[way, :, half * 128 : half * 128 + 128] = tile
        pass_gates[way].start()

    for copy in lead:
        copy.wait_recv()
    for copy in pass_on:
        copy.wait_recv()
    reach = (jnp.where(me_x > 0, 1.0, 0.0), jnp.where(me_x < size_x - 1, 1.0, 0.0))
    outer_mask = jnp.zeros((16, 128), jnp.float32)
    outer_far_mask = jnp.zeros((16, 128), jnp.float32)
    outer_first = jnp.zeros((16, 128), jnp.float32)
    for way, (edge, inward, slot, far) in enumerate(((7, 6, 1, 0), (0, 1, 10, 11))):
        for half in range(2):
            columns = slice(half * 128, half * 128 + 128)
            for plane, target in ((edge, slot), (inward, far)):
                index = 512 + 2 * plane + half
                mask[target, :, columns] = (
                    jnp.broadcast_to(first_in[way, :, index : index + 1], (16, 128)) * reach[way]
                )
        cells[0, slot - 1] = first_in[way, :, 256:512]
        packed[0, slot] = mask[slot] * first_in[way, :, 256:512]
        hop_in[way, 0, :, 0:256] = first_in[way, :, 0:256]
        place = way * 16
        here = (lane >= place) & (lane < place + 16)
        relayed = relay_in[way]
        outer_first = jnp.where(here, turn(relayed, place), outer_first)
        outer_mask = jnp.where(here, turn(relayed, place - 16) * reach[way], outer_mask)
        outer_far_mask = jnp.where(here, turn(relayed, place - 32) * reach[way], outer_far_mask)
        hop_in[way, 0, :, 256:384] = turn(relayed, inward * 16 - 48)
    strip_cells[1, 0] = outer_first
    strip_mask[1] = outer_mask
    strip_packed[0, 1] = outer_mask * outer_first

    def inner_sums(read, strip, outer, planes, emit, emit_strip):
        factors = [coef[index] for index in range(9)]
        shifts, edges = {}, {}
        for plane in range(min(planes) - 1, max(planes) + 2):
            tiles = read(plane)
            if 0 <= plane < INNER:
                shifts[plane] = plane_shifts(*tiles, strip, plane * 16)
            else:
                shifts[plane] = plane_shifts(*tiles, outer, 0 if plane < 0 else 16)
            edges[plane] = tiles
        if emit_strip is not None:
            inner = strip_shifts(strip, [(16 * p, *edges[p]) for p in range(INNER)])
            rim = strip_shifts(outer, [(0, *edges[-1]), (16, *edges[INNER])])
            up = [
                jnp.where(lane >= 112, turn(beyond, 96), turn(part, 112))
                for part, beyond in zip(inner, rim)
            ]
            down = [
                jnp.where(lane < 16, beyond, turn(part, 16)) for part, beyond in zip(inner, rim)
            ]
            emit_strip(tile_sum(factors, inner, up, down))
        for plane in planes:
            for half in range(2):
                total = tile_sum(
                    factors,
                    shifts[plane][half],
                    shifts[plane + 1][half],
                    shifts[plane - 1][half],
                )
                emit(plane, half, total)

    def outer_sums(read, strip, outer, far, emit, emit_strip):
        factors = [coef[index] for index in range(9)]
        rims, insides, fars = [], [], []
        far_tile = jnp.zeros((16, 128), jnp.float32)
        far_edges, rim_edges = [], []
        near_tile = jnp.where(lane < 16, strip, turn(strip, 32))
        near_edges = []
        for way, (rim, near) in enumerate(((-1, 0), (INNER, INNER - 1))):
            rim_tiles, near_tiles = read(rim), read(near)
            first, second, far_strip, base = far(way)
            rims.append(plane_shifts(*rim_tiles, outer, way * 16))
            insides.append(plane_shifts(*near_tiles, strip, near * 16))
            fars.append(plane_shifts(first, second, far_strip, base))
            place = way * 16
            here = (lane >= place) & (lane < place + 16)
            far_tile = jnp.where(here, turn(far_strip, place - base), far_tile)
            far_edges.append((place, first, second))
            rim_edges.append((place, *rim_tiles))
            near_edges.append((place, *near_tiles))
        rim = strip_shifts(outer, rim_edges)
        near = strip_shifts(near_tile, near_edges)
        far_shift = strip_shifts(far_tile, far_edges)
        lower = lane < 16
        up = [jnp.where(lower, a, b) for a, b in zip(near, far_shift)]
        down = [jnp.where(lower, b, a) for a, b in zip(near, far_shift)]
        emit_strip(tile_sum(factors, rim, up, down))
        for way, plane in enumerate((-1, INNER)):
            for half in range(2):
                toward, away = insides[way][half], fars[way][half]
                pair = (toward, away) if way == 0 else (away, toward)
                emit(plane, half, tile_sum(factors, rims[way][half], *pair))

    def mask_tiles(plane):
        return mask[plane + 2, :, 0:128], mask[plane + 2, :, 128:256]

    def keep_plane(plane, half, total):
        columns = slice(half * 128, half * 128 + 128)
        keep[plane + 1, :, columns] = 1.0 - mask[plane + 2, :, columns] * total

    def keep_strip(which):
        def emit(total):
            strip_keep[which] = 1.0 - strip_mask[which] * total

        return emit

    inner_sums(
        mask_tiles, strip_mask[0], strip_mask[1], range(INNER), keep_plane, keep_strip(0)
    )
    outer_sums(
        mask_tiles,
        strip_mask[0],
        strip_mask[1],
        lambda way: (*mask_tiles(-2 if way == 0 else 9), outer_far_mask, way * 16),
        keep_plane,
        keep_strip(1),
    )

    def move_plane(plane, half, total):
        columns = slice(half * 128, half * 128 + 128)
        cells[0, plane + 1, :, columns] = (
            cells[0, plane + 1, :, columns] * keep[plane + 1, :, columns]
            + mask[plane + 2, :, columns] * total
        )

    def move_strip(which):
        def emit(total):
            strip_cells[which, 0] = (
                strip_cells[which, 0] * strip_keep[which] + strip_mask[which] * total
            )

        return emit

    def packed_tiles(parity):
        return lambda plane: (
            packed[parity, plane + 2, :, 0:128],
            packed[parity, plane + 2, :, 128:256],
        )

    def hop(way, step):
        return remote(
            hop_out.at[way, lax.rem(step, 2)],
            hop_in.at[way, step],
            hop_send.at[way, step],
            hop_recv.at[way, step],
            along_x[way],
        )

    def advance(step, carry):
        now = lax.rem(step, 2)
        old = 1 - now
        inner_sums(
            packed_tiles(old),
            strip_packed[old, 0],
            strip_packed[old, 1],
            range(INNER),
            move_plane,
            move_strip(0),
        )
        react_strip(0, now)
        react_pair(1, 0, now)

        @pl.when(step < HOPS)
        def _():
            @pl.when(step > 2)
            def _():
                for way in range(2):
                    hop(way, step - 2).wait_send()

            for way, inward in enumerate((6, 1)):
                hop_out[way, now, :, 0:256] = packed[now, inward + 2]
                hop_out[way, now, :, 256:384] = strip_packed[now, 0]
                hop(way, step).start()

        lax.fori_loop(2, 4, lambda pair, kept: react_pair(pair, kept, now), 0)
        react_pair(0, 0, now)

        @pl.when(step == 1)
        def _():
            for copy in bulk:
                copy.wait_recv()
            for copy in pass_gates:
                copy.wait_recv()
            for half, gates in enumerate((range(1, 9), range(9, 12))):
                for group, comp in enumerate(gates):
                    tile = jnp.zeros((16, 128), jnp.float32)
                    for way in range(2):
                        place = way * 16
                        here = (lane >= place) & (lane < place + 16)
                        source = relay_gates_in[way, :, half * 128 : half * 128 + 128]
                        tile = jnp.where(here, turn(source, place - group * 16), tile)
                    strip_cells[1, comp] = tile

        @pl.when(step > 1)
        def _():
            for way in range(2):
                hop(way, step - 1).wait_recv()

        outer_sums(
            packed_tiles(old),
            strip_packed[old, 0],
            strip_packed[old, 1],
            lambda way: (
                hop_in[way, step - 1, :, 0:128],
                hop_in[way, step - 1, :, 128:256],
                hop_in[way, step - 1, :, 256:384],
                96 if way == 0 else 16,
            ),
            move_plane,
            move_strip(1),
        )
        react_strip(1, now)
        react_plane(0, now)
        react_plane(9, now)
        return carry

    lax.fori_loop(1, STEPS, advance, 0)

    stores = [
        pltpu.make_async_copy(
            cells.at[pl.ds(1, 11), pl.ds(1, INNER)], out_ref.at[pl.ds(1, 11)], store_sem.at[0]
        ),
        pltpu.make_async_copy(cells.at[0, pl.ds(1, INNER)], out_ref.at[0], store_sem.at[1]),
    ]
    stores[0].start()
    last = (STEPS - 1) % 2
    inner_sums(
        packed_tiles(last),
        strip_packed[last, 0],
        strip_packed[last, 1],
        range(INNER),
        move_plane,
        None,
    )
    stores[1].start()
    for copies in (early, lead, late, bulk, pass_on, pass_gates):
        for copy in copies:
            copy.wait_send()
    for way in range(2):
        for step in (HOPS - 2, HOPS - 1):
            hop(way, step).wait_send()
    for copy in stores:
        copy.wait()


def shards(state, tissue_mask, layer_index, fibre):
    vmem, sems = pltpu.VMEM, pltpu.SemaphoreType.DMA
    f32 = jnp.float32
    return pl.pallas_call(
        kernel,
        out_shape=jax.ShapeDtypeStruct(state.shape, f32),
        in_specs=[
            pl.BlockSpec(memory_space=pl.ANY),
            pl.BlockSpec(memory_space=pltpu.VMEM),
            pl.BlockSpec(memory_space=pltpu.SMEM),
            pl.BlockSpec(memory_space=pltpu.SMEM),
        ],
        out_specs=pl.BlockSpec(memory_space=pl.ANY),
        scratch_shapes=[
            vmem((COMPS, 10, 16, 256), f32),
            vmem((2, 12, 16, 256), f32),
            vmem((10, 16, 256), f32),
            vmem((12, 16, 256), f32),
            vmem((2, COMPS, 16, 128), f32),
            vmem((2, 2, 16, 128), f32),
            vmem((2, 16, 128), f32),
            vmem((2, 16, 128), f32),
            vmem((9, 16, 128), f32),
            vmem((2, 2, 16, 384), f32),
            vmem((2, HOPS, 16, 384), f32),
            vmem((2, 16, 640), f32),
            vmem((2, 16, 640), f32),
            vmem((2, 11, 16, 256), f32),
            vmem((13, 16, 128), f32),
            vmem((2, 13, 16, 128), f32),
            vmem((2, 16, 128), f32),
            vmem((2, 16, 128), f32),
            vmem((2, 16, 256), f32),
            vmem((2, 16, 256), f32),
            sems((2, HOPS)),
            sems((2, HOPS)),
            sems((2,)),
            sems((2,)),
            sems((2,)),
            sems((2,)),
            sems((2, 2)),
            sems((2, 2)),
            sems((2, 2)),
            sems((2, 2)),
            sems((INNER,)),
            sems((2,)),
        ],
        compiler_params=pltpu.CompilerParams(collective_id=0, has_side_effects=True),
        name="slab",
    )(state, tissue_mask, layer_index, fibre)


def solution(mesh):
    placed = (P(None, "gx", None, "gy"), P("gx", None, "gy"), P(), P())
    return jax.shard_map(
        shards, mesh=mesh, in_specs=placed, out_specs=P(None, "gx", None, "gy"), check_vma=False
    )
```

time: 268 us -> 49.9 us (0.19)
  the two profiles are of different devices: /device:TPU:91 before, /device:TPU:6 now
where the time goes in v1:
time: 49.9 us; the launch traced here: 49.7 us
  Pallas kernels  45.5 us (91%)
  local copies, waits for them, and re-layouts  4.11 us (8%)
    pallas_call x1, Pallas kernels, shards(): pl.pallas_call(kernel, out_shape=jax.ShapeDtypeStruct(state.shape, f32),...  45.5 us
    unnamed x2, local copies, waits for them, and re-layouts  4.11 us

profile of v1, /device:TPU:6, one launch (start us, length us, event | category | flops | bytes accessed | tf_op | source)
XLA Modules:
  0.0 49.7 jit_solution(9912724372478529081)
XLA Ops:
  0.0 1.4 %copy.5.mask_ref = s32[8,16,2]{2,1,0:T(8,128)} copy(s32[8,16,2]{1,2,0:T(2,128)} %param.5) | data formatting | bytes 2048 | tf_op args[1]
  1.4 45.5 %slab.1 = f32[12,8,16,256]{3,2,1,0:T(8,128)} custom-call(f32[12,8,16,256]{3,2,1,0:T(8,128)} %state_ref.1, s32[8,16,2]{2,1,0:T(8,128)} %copy.5.mask_ref, s32[16]{0:T(128)} %layer_ref.1, f32[2,8]{1,0:T(2,128)} %fibre_ref.1), custom_call_target="tpu_custom_call" | custom-call | tf_op jit(solution)/shard_map/slab/pallas_call | solution.py:708
  47.0 2.7 %copy.7 = f32[12,8,16,256]{3,2,1,0:T(8,128)} copy(f32[12,8,16,256]{3,2,1,0:T(8,128)} %slab.1) | data formatting | bytes 3145728

commit v2 on v1

--- a/solution.py
+++ b/solution.py
@@ -244,12 +244,12 @@
     strip_packed,
     strip_keep,
     strip_mask,
+    far_mask,
     coef,
-    hop_out,
     hop_in,
-    first_out,
-    first_in,
-    gates_out,
+    hop_strip_in,
+    spread_out,
+    spread_in,
     side_out,
     side_in,
     relay_out,
@@ -258,10 +258,10 @@
     relay_gates_in,
     hop_send,
     hop_recv,
-    first_send,
-    first_recv,
-    gates_send,
-    gates_recv,
+    strip_send,
+    strip_recv,
+    lead_send,
+    lead_recv,
     side_send,
     side_recv,
     relay_send,
@@ -271,16 +271,26 @@
 ):
     me_x, me_y = lax.axis_index("gx"), lax.axis_index("gy")
     size_x, size_y = lax.axis_size("gx"), lax.axis_size("gy")
-    above = lax.rem(me_x + 1, size_x)
-    below = lax.rem(me_x + size_x - 1, size_x)
-    right = lax.rem(me_y + 1, size_y)
-    left = lax.rem(me_y + size_y - 1, size_y)
-    along_x = ((above, me_y), (below, me_y))
-    along_y = ((me_x, right), (me_x, left))
+    along_x = ((me_x + 1, me_y), (me_x - 1, me_y))
+    along_y = ((me_x, me_y + 1), (me_x, me_y - 1))
+    ends_x = (me_x < size_x - 1, me_x > 0)
+    ends_y = (me_y < size_y - 1, me_y > 0)
+    ways = (0, 1)
+
+    def sending(ends, way, action):
+        pl.when(ends[way])(action)
+
+    def receiving(ends, way, action):
+        pl.when(ends[1 - way])(action)
 
     barrier = pltpu.get_barrier_semaphore()
-    for target in along_x + along_y:
-        pl.semaphore_signal(barrier, inc=1, device_id=target, device_id_type=MESH)
+    for ends, targets in ((ends_x, along_x), (ends_y, along_y)):
+        for way in ways:
+
+            def greet(target=targets[way]):
+                pl.semaphore_signal(barrier, inc=1, device_id=target, device_id_type=MESH)
+
+            sending(ends, way, greet)
 
     def remote(source, target, sends, recvs, device):
         return pltpu.make_async_remote_copy(
@@ -302,12 +312,39 @@
     lane = lanes()
     coefficients(layer_ref, fibre_ref, coef)
     spread_tile = jnp.zeros((16, 128), jnp.float32)
+    unit = (
+        lax.broadcasted_iota(jnp.int32, (16, 16), 0) == lax.broadcasted_iota(jnp.int32, (16, 16), 1)
+    ).astype(jnp.float32)
     for plane in range(INNER):
-        blocks = (mask_ref[plane] > 0).astype(jnp.float32)
+        blocks = lax.dot_general(
+            unit,
+            (mask_ref[plane] > 0).astype(jnp.float32),
+            (((1,), (1,)), ((), ())),
+            preferred_element_type=jnp.float32,
+        )
         for half in range(2):
             tile = jnp.broadcast_to(blocks[:, half : half + 1], (16, 128))
             mask[plane + 2, :, half * 128 : half * 128 + 128] = tile
             spread_tile = jnp.where(lane == 2 * plane + half, tile, spread_tile)
+    spread_out[...] = spread_tile
+
+    for way in ways:
+
+        @pl.when(jnp.logical_not(ends_x[1 - way]))
+        def _(way=way):
+            for step in range(HOPS):
+                hop_in[way, step] = jnp.zeros((16, 256), jnp.float32)
+                hop_strip_in[way, step] = jnp.zeros((16, 128), jnp.float32)
+            spread_in[way] = jnp.zeros((16, 128), jnp.float32)
+            relay_in[way] = jnp.zeros((16, 128), jnp.float32)
+            relay_gates_in[way] = jnp.zeros((16, 256), jnp.float32)
+            for comp in range(COMPS):
+                cells[comp, 0 if way == 0 else 9] = jnp.zeros((16, 256), jnp.float32)
+
+        @pl.when(jnp.logical_not(ends_y[1 - way]))
+        def _(way=way):
+            for comp in range(COMPS + 1):
+                side_in[way, comp] = jnp.zeros((16, 128), jnp.float32)
 
     def react_plane(slot, parity):
         for top in (0, 8):
@@ -327,22 +364,18 @@
                 strip_cells[which, comp, rows] = fresh[comp]
             strip_packed[parity, which, rows] = jnp.where(inside, fresh[0], 0.0)
 
-    def react_pair(pair, carry, parity):
+    def react_pair(pair, parity):
         react_plane(pair + 1, parity)
         react_plane(8 - pair, parity)
+
+    for copy in loads:
+        copy.wait()
+
+    def first_pair(pair, carry):
+        react_pair(pair, 0)
         return carry
 
-    for pair in range(4):
-        loads[pair].wait()
-        loads[7 - pair].wait()
-
-    lax.fori_loop(0, 4, lambda pair, carry: react_pair(pair, carry, 0), 0)
-
-    for way, (edge, inward) in enumerate(((7, 6), (0, 1))):
-        first_out[way, :, 0:256] = packed[0, inward + 2]
-        first_out[way, :, 256:512] = cells[0, edge + 1]
-        first_out[way, :, 512:640] = spread_tile
-        gates_out[way] = cells[1:12, edge + 1]
+    lax.fori_loop(0, 4, first_pair, 0)
 
     def pack_side(read):
         tile = jnp.zeros((16, 128), jnp.float32)
@@ -361,9 +394,11 @@
     for comp in range(1, COMPS):
         side_out[comp + 1] = pack_side(own(comp))
 
-    pl.semaphore_wait(barrier, 4)
-    early, late, lead, bulk, pass_on, pass_gates = [], [], [], [], [], []
-    for way in range(2):
+    peers = sum(end.astype(jnp.int32) for end in ends_x + ends_y)
+    pl.semaphore_wait(barrier, peers)
+
+    early, late, lead, bulk, relay, relay_gates = [], [], [], [], [], []
+    for way, (edge, inward, slot) in enumerate(((7, 6, 0), (0, 1, 9))):
         early.append(
             remote(
                 side_out.at[pl.ds(0, 2)],
@@ -373,15 +408,6 @@
                 along_y[way],
             )
         )
-        lead.append(
-            remote(
-                first_out.at[way],
-                first_in.at[way],
-                first_send.at[way],
-                first_recv.at[way],
-                along_x[way],
-            )
-        )
         late.append(
             remote(
                 side_out.at[pl.ds(2, 11)],
@@ -391,16 +417,33 @@
                 along_y[way],
             )
         )
+        lead.append(
+            [
+                remote(
+                    source, target, lead_send.at[index, way], lead_recv.at[index, way], along_x[way]
+                )
+                for index, (source, target) in enumerate(
+                    (
+                        (cells.at[0, edge + 1], cells.at[0, slot]),
+                        (packed.at[0, inward + 2], hop_in.at[way, 0]),
+                        (spread_out, spread_in.at[way]),
+                    )
+                )
+            ]
+        )
         bulk.append(
-            remote(
-                gates_out.at[way],
-                cells.at[pl.ds(1, 11), 0 if way == 0 else 9],
-                gates_send.at[way],
-                gates_recv.at[way],
-                along_x[way],
-            )
-        )
-        pass_on.append(
+            [
+                remote(
+                    cells.at[pl.ds(start, size), edge + 1],
+                    cells.at[pl.ds(start, size), slot],
+                    lead_send.at[index, way],
+                    lead_recv.at[index, way],
+                    along_x[way],
+                )
+                for index, start, size in ((3, 1, 5), (4, 6, 6))
+            ]
+        )
+        relay.append(
             remote(
                 relay_out.at[way],
                 relay_in.at[way],
@@ -409,7 +452,7 @@
                 along_x[way],
             )
         )
-        pass_gates.append(
+        relay_gates.append(
             remote(
                 relay_gates_out.at[way],
                 relay_gates_in.at[way],
@@ -418,17 +461,20 @@
                 along_x[way],
             )
         )
-    for copies in (early, lead, late, bulk):
-        for copy in copies:
-            copy.start()
+    for way in ways:
+        sending(ends_y, way, early[way].start)
+    for way in ways:
+        for copy in lead[way]:
+            sending(ends_x, way, copy.start)
+    for way in ways:
+        sending(ends_y, way, late[way].start)
+        sending(ends_x, way, bulk[way][0].start)
 
     from_left = lax.rem(lane, 16) < 8
-    for copy in early:
-        copy.wait_recv()
+    for way in ways:
+        receiving(ends_y, way, early[way].wait_recv)
     strip_cells[0, 0] = jnp.where(from_left, side_in[0, 0], side_in[1, 0])
-    reach_left = jnp.where(me_y > 0, 1.0, 0.0)
-    reach_right = jnp.where(me_y < size_y - 1, 1.0, 0.0)
-    strip_mask[0] = jnp.where(from_left, side_in[0, 1] * reach_left, side_in[1, 1] * reach_right)
+    strip_mask[0] = jnp.where(from_left, side_in[0, 1], side_in[1, 1])
     strip_packed[0, 0] = strip_mask[0] * strip_cells[0, 0]
     for way, (edge, inward) in enumerate(((7, 6), (0, 1))):
         tile = jnp.zeros((16, 128), jnp.float32)
@@ -442,72 +488,20 @@
             here = (lane >= group * 16) & (lane < group * 16 + 16)
             tile = jnp.where(here, turn(part, group * 16 - plane * 16), tile)
         relay_out[way] = tile
-        pass_on[way].start()
-
-    for copy in late:
-        copy.wait_recv()
-    for comp in range(1, COMPS):
-        strip_cells[0, comp] = jnp.where(from_left, side_in[0, comp + 1], side_in[1, comp + 1])
-    for way, edge in enumerate((7, 0)):
-        for half, gates in enumerate((range(1, 9), range(9, 12))):
-            tile = jnp.zeros((16, 128), jnp.float32)
-            for group, comp in enumerate(gates):
-                here = (lane >= group * 16) & (lane < group * 16 + 16)
-                tile = jnp.where(here, turn(strip_cells[0, comp], group * 16 - edge * 16), tile)
-            relay_gates_out[way, :, half * 128 : half * 128 + 128] = tile
-        pass_gates[way].start()
-
-    for copy in lead:
-        copy.wait_recv()
-    for copy in pass_on:
-        copy.wait_recv()
-    reach = (jnp.where(me_x > 0, 1.0, 0.0), jnp.where(me_x < size_x - 1, 1.0, 0.0))
-    outer_mask = jnp.zeros((16, 128), jnp.float32)
-    outer_far_mask = jnp.zeros((16, 128), jnp.float32)
-    outer_first = jnp.zeros((16, 128), jnp.float32)
-    for way, (edge, inward, slot, far) in enumerate(((7, 6, 1, 0), (0, 1, 10, 11))):
-        for half in range(2):
-            columns = slice(half * 128, half * 128 + 128)
-            for plane, target in ((edge, slot), (inward, far)):
-                index = 512 + 2 * plane + half
-                mask[target, :, columns] = (
-                    jnp.broadcast_to(first_in[way, :, index : index + 1], (16, 128)) * reach[way]
-                )
-        cells[0, slot - 1] = first_in[way, :, 256:512]
-        packed[0, slot] = mask[slot] * first_in[way, :, 256:512]
-        hop_in[way, 0, :, 0:256] = first_in[way, :, 0:256]
-        place = way * 16
-        here = (lane >= place) & (lane < place + 16)
-        relayed = relay_in[way]
-        outer_first = jnp.where(here, turn(relayed, place), outer_first)
-        outer_mask = jnp.where(here, turn(relayed, place - 16) * reach[way], outer_mask)
-        outer_far_mask = jnp.where(here, turn(relayed, place - 32) * reach[way], outer_far_mask)
-        hop_in[way, 0, :, 256:384] = turn(relayed, inward * 16 - 48)
-    strip_cells[1, 0] = outer_first
-    strip_mask[1] = outer_mask
-    strip_packed[0, 1] = outer_mask * outer_first
-
-    def inner_sums(read, strip, outer, planes, emit, emit_strip):
-        factors = [coef[index] for index in range(9)]
-        shifts, edges = {}, {}
-        for plane in range(min(planes) - 1, max(planes) + 2):
-            tiles = read(plane)
-            if 0 <= plane < INNER:
-                shifts[plane] = plane_shifts(*tiles, strip, plane * 16)
-            else:
-                shifts[plane] = plane_shifts(*tiles, outer, 0 if plane < 0 else 16)
-            edges[plane] = tiles
-        if emit_strip is not None:
-            inner = strip_shifts(strip, [(16 * p, *edges[p]) for p in range(INNER)])
-            rim = strip_shifts(outer, [(0, *edges[-1]), (16, *edges[INNER])])
-            up = [
-                jnp.where(lane >= 112, turn(beyond, 96), turn(part, 112))
-                for part, beyond in zip(inner, rim)
-            ]
-            down = [
-                jnp.where(lane < 16, beyond, turn(part, 16)) for part, beyond in zip(inner, rim)
-            ]
-            emit_strip(tile_sum(factors, inner, up, down))
+        sending(ends_x, way, relay[way].start)
+        sending(ends_x, way, bulk[way][1].start)
+
+    def base_of(plane):
+        return (0, plane * 16) if 0 <= plane < INNER else (1, 0 if plane < 0 else 16)
+
+    def shift_planes(read, strips, planes):
+        shifts = {}
+        for plane in planes:
+            which, base = base_of(plane)
+            shifts[plane] = plane_shifts(*read(plane), strips[which], base)
+        return shifts
+
+    def emit_planes(factors, shifts, planes, emit):
         for plane in planes:
             for half in range(2):
                 total = tile_sum(
@@ -518,37 +512,52 @@
                 )
                 emit(plane, half, total)
 
-    def outer_sums(read, strip, outer, far, emit, emit_strip):
-        factors = [coef[index] for index in range(9)]
-        rims, insides, fars = [], [], []
+    def load_factors():
+        return [coef[index] for index in range(9)]
+
+    def inner_sums(read, strips, emit):
+        shifts = shift_planes(read, strips, range(INNER))
+        emit_planes(load_factors(), shifts, range(1, INNER - 1), emit)
+
+    def strip_sums(read, strips, emit_strip):
+        inner = strip_shifts(strips[0], [(16 * p, *read(p)) for p in range(INNER)])
+        rim = strip_shifts(strips[1], [(0, *read(-1)), (16, *read(INNER))])
+        up = [
+            jnp.where(lane >= 112, turn(beyond, 96), turn(part, 112))
+            for part, beyond in zip(inner, rim)
+        ]
+        down = [jnp.where(lane < 16, beyond, turn(part, 16)) for part, beyond in zip(inner, rim)]
+        emit_strip(tile_sum(load_factors(), inner, up, down))
+
+    def edge_sums(read, strips, emit):
+        shifts = shift_planes(read, strips, (-1, 0, 1, 6, 7, 8))
+        emit_planes(load_factors(), shifts, (0, 7), emit)
+
+    def rim_strip_sums(read, strips, far, emit_strip):
         far_tile = jnp.zeros((16, 128), jnp.float32)
-        far_edges, rim_edges = [], []
-        near_tile = jnp.where(lane < 16, strip, turn(strip, 32))
-        near_edges = []
+        far_edges, rim_edges, near_edges = [], [], []
         for way, (rim, near) in enumerate(((-1, 0), (INNER, INNER - 1))):
-            rim_tiles, near_tiles = read(rim), read(near)
             first, second, far_strip, base = far(way)
-            rims.append(plane_shifts(*rim_tiles, outer, way * 16))
-            insides.append(plane_shifts(*near_tiles, strip, near * 16))
-            fars.append(plane_shifts(first, second, far_strip, base))
             place = way * 16
             here = (lane >= place) & (lane < place + 16)
             far_tile = jnp.where(here, turn(far_strip, place - base), far_tile)
             far_edges.append((place, first, second))
-            rim_edges.append((place, *rim_tiles))
-            near_edges.append((place, *near_tiles))
-        rim = strip_shifts(outer, rim_edges)
+            rim_edges.append((place, *read(rim)))
+            near_edges.append((place, *read(near)))
+        near_tile = jnp.where(lane < 16, strips[0], turn(strips[0], 32))
+        rim = strip_shifts(strips[1], rim_edges)
         near = strip_shifts(near_tile, near_edges)
-        far_shift = strip_shifts(far_tile, far_edges)
+        beyond = strip_shifts(far_tile, far_edges)
         lower = lane < 16
-        up = [jnp.where(lower, a, b) for a, b in zip(near, far_shift)]
-        down = [jnp.where(lower, b, a) for a, b in zip(near, far_shift)]
-        emit_strip(tile_sum(factors, rim, up, down))
-        for way, plane in enumerate((-1, INNER)):
-            for half in range(2):
-                toward, away = insides[way][half], fars[way][half]
-                pair = (toward, away) if way == 0 else (away, toward)
-                emit(plane, half, tile_sum(factors, rims[way][half], *pair))
+        up = [jnp.where(lower, a, b) for a, b in zip(near, beyond)]
+        down = [jnp.where(lower, b, a) for a, b in zip(near, beyond)]
+        emit_strip(tile_sum(load_factors(), rim, up, down))
+
+    def rim_sums(read, strips, far, emit):
+        shifts = shift_planes(read, strips, (-1, 0, 7, 8))
+        shifts[-2] = plane_shifts(*far(0))
+        shifts[9] = plane_shifts(*far(1))
+        emit_planes(load_factors(), shifts, (-1, INNER), emit)
 
     def mask_tiles(plane):
         return mask[plane + 2, :, 0:128], mask[plane + 2, :, 128:256]
@@ -563,17 +572,8 @@
 
         return emit
 
-    inner_sums(
-        mask_tiles, strip_mask[0], strip_mask[1], range(INNER), keep_plane, keep_strip(0)
-    )
-    outer_sums(
-        mask_tiles,
-        strip_mask[0],
-        strip_mask[1],
-        lambda way: (*mask_tiles(-2 if way == 0 else 9), outer_far_mask, way * 16),
-        keep_plane,
-        keep_strip(1),
-    )
+    def mask_far(way):
+        return (*mask_tiles(-2 if way == 0 else 9), far_mask[...], way * 16)
 
     def move_plane(plane, half, total):
         columns = slice(half * 128, half * 128 + 128)
@@ -590,87 +590,173 @@
 
         return emit
 
-    def packed_tiles(parity):
+    def tiles(parity):
         return lambda plane: (
             packed[parity, plane + 2, :, 0:128],
             packed[parity, plane + 2, :, 128:256],
         )
 
-    def hop(way, step):
+    def strips_of(parity):
+        return strip_packed[parity, 0], strip_packed[parity, 1]
+
+    def hop(way, step, parity):
         return remote(
-            hop_out.at[way, lax.rem(step, 2)],
+            packed.at[parity, 8 if way == 0 else 3],
             hop_in.at[way, step],
             hop_send.at[way, step],
             hop_recv.at[way, step],
             along_x[way],
         )
 
+    def strip_hop(way, step, parity):
+        return remote(
+            strip_packed.at[parity, 0],
+            hop_strip_in.at[way, step],
+            strip_send.at[way, step],
+            strip_recv.at[way, step],
+            along_x[way],
+        )
+
+    def rim_step(step, parity):
+        def far(way):
+            return (
+                hop_in[way, step - 1, :, 0:128],
+                hop_in[way, step - 1, :, 128:256],
+                hop_strip_in[way, step - 1],
+                96 if way == 0 else 16,
+            )
+
+        read, strips = tiles(parity), strips_of(parity)
+        rim_strip_sums(read, strips, far, move_strip(1))
+        rim_sums(read, strips, far, move_plane)
+        react_strip(1, 1 - parity)
+
+    def rim_planes(parity):
+        react_plane(0, parity)
+        react_plane(9, parity)
+
+    def open_rim():
+        for way in ways:
+            for copy in lead[way]:
+                receiving(ends_x, way, copy.wait_recv)
+            receiving(ends_x, way, relay[way].wait_recv)
+        outer_mask = jnp.zeros((16, 128), jnp.float32)
+        outer_far_mask = jnp.zeros((16, 128), jnp.float32)
+        outer_first = jnp.zeros((16, 128), jnp.float32)
+        for way, (edge, inward, slot, beyond) in enumerate(((7, 6, 1, 0), (0, 1, 10, 11))):
+            for half in range(2):
+                columns = slice(half * 128, half * 128 + 128)
+                for plane, target in ((edge, slot), (inward, beyond)):
+                    index = 2 * plane + half
+                    mask[target, :, columns] = jnp.broadcast_to(
+                        spread_in[way, :, index : index + 1], (16, 128)
+                    )
+            packed[0, slot] = mask[slot] * cells[0, slot - 1]
+            place = way * 16
+            here = (lane >= place) & (lane < place + 16)
+            relayed = relay_in[way]
+            outer_first = jnp.where(here, turn(relayed, place), outer_first)
+            outer_mask = jnp.where(here, turn(relayed, place - 16), outer_mask)
+            outer_far_mask = jnp.where(here, turn(relayed, place - 32), outer_far_mask)
+            hop_strip_in[way, 0] = turn(relayed, inward * 16 - 48)
+        strip_cells[1, 0] = outer_first
+        strip_mask[1] = outer_mask
+        strip_packed[0, 1] = outer_mask * outer_first
+        far_mask[...] = outer_far_mask
+        masks = (strip_mask[0], outer_mask)
+        strip_sums(mask_tiles, masks, keep_strip(0))
+        edge_sums(mask_tiles, masks, keep_plane)
+        rim_strip_sums(mask_tiles, masks, mask_far, keep_strip(1))
+        rim_sums(mask_tiles, masks, mask_far, keep_plane)
+
+    def open_rim_gates():
+        for way in ways:
+            for copy in bulk[way]:
+                receiving(ends_x, way, copy.wait_recv)
+            receiving(ends_x, way, relay_gates[way].wait_recv)
+        for half, gates in enumerate((range(1, 9), range(9, 12))):
+            for group, comp in enumerate(gates):
+                tile = jnp.zeros((16, 128), jnp.float32)
+                for way in ways:
+                    place = way * 16
+                    here = (lane >= place) & (lane < place + 16)
+                    source = relay_gates_in[way, :, half * 128 : half * 128 + 128]
+                    tile = jnp.where(here, turn(source, place - group * 16), tile)
+                strip_cells[1, comp] = tile
+
+    def open_strip_gates():
+        for way in ways:
+            receiving(ends_y, way, late[way].wait_recv)
+        for comp in range(1, COMPS):
+            strip_cells[0, comp] = jnp.where(from_left, side_in[0, comp + 1], side_in[1, comp + 1])
+        for way, edge in enumerate((7, 0)):
+            for half, gates in enumerate((range(1, 9), range(9, 12))):
+                tile = jnp.zeros((16, 128), jnp.float32)
+                for group, comp in enumerate(gates):
+                    here = (lane >= group * 16) & (lane < group * 16 + 16)
+                    tile = jnp.where(here, turn(strip_cells[0, comp], group * 16 - edge * 16), tile)
+                relay_gates_out[way, :, half * 128 : half * 128 + 128] = tile
+            sending(ends_x, way, relay_gates[way].start)
+
+    inner_sums(mask_tiles, (strip_mask[0], None), keep_plane)
+
     def advance(step, carry):
         now = lax.rem(step, 2)
         old = 1 - now
-        inner_sums(
-            packed_tiles(old),
-            strip_packed[old, 0],
-            strip_packed[old, 1],
-            range(INNER),
-            move_plane,
-            move_strip(0),
-        )
-        react_strip(0, now)
-        react_pair(1, 0, now)
+
+        @pl.when(step > 2)
+        def _():
+            for way in ways:
+                sending(ends_x, way, hop(way, step - 2, now).wait_send)
+
+        inner_sums(tiles(old), strips_of(old), move_plane)
+        react_pair(1, now)
 
         @pl.when(step < HOPS)
         def _():
-            @pl.when(step > 2)
-            def _():
-                for way in range(2):
-                    hop(way, step - 2).wait_send()
-
-            for way, inward in enumerate((6, 1)):
-                hop_out[way, now, :, 0:256] = packed[now, inward + 2]
-                hop_out[way, now, :, 256:384] = strip_packed[now, 0]
-                hop(way, step).start()
-
-        lax.fori_loop(2, 4, lambda pair, kept: react_pair(pair, kept, now), 0)
-        react_pair(0, 0, now)
+            for way in ways:
+                sending(ends_x, way, hop(way, step, now).start)
+
+        def pairs(pair, kept):
+            react_pair(pair, now)
+            return kept
+
+        lax.fori_loop(2, 4, pairs, 0)
 
         @pl.when(step == 1)
         def _():
-            for copy in bulk:
-                copy.wait_recv()
-            for copy in pass_gates:
-                copy.wait_recv()
-            for half, gates in enumerate((range(1, 9), range(9, 12))):
-                for group, comp in enumerate(gates):
-                    tile = jnp.zeros((16, 128), jnp.float32)
-                    for way in range(2):
-                        place = way * 16
-                        here = (lane >= place) & (lane < place + 16)
-                        source = relay_gates_in[way, :, half * 128 : half * 128 + 128]
-                        tile = jnp.where(here, turn(source, place - group * 16), tile)
-                    strip_cells[1, comp] = tile
+            open_strip_gates()
+            open_rim()
+            for way in ways:
+                for copy in lead[way] + bulk[way]:
+                    sending(ends_x, way, copy.wait_send)
+
+        @pl.when(step == 2)
+        def _():
+            open_rim_gates()
+
+        @pl.when(step > 2)
+        def _():
+            for way in ways:
+                for copy in (hop(way, step - 2, now), strip_hop(way, step - 2, now)):
+                    receiving(ends_x, way, copy.wait_recv)
+                sending(ends_x, way, strip_hop(way, step - 2, now).wait_send)
 
         @pl.when(step > 1)
         def _():
-            for way in range(2):
-                hop(way, step - 1).wait_recv()
-
-        outer_sums(
-            packed_tiles(old),
-            strip_packed[old, 0],
-            strip_packed[old, 1],
-            lambda way: (
-                hop_in[way, step - 1, :, 0:128],
-                hop_in[way, step - 1, :, 128:256],
-                hop_in[way, step - 1, :, 256:384],
-                96 if way == 0 else 16,
-            ),
-            move_plane,
-            move_strip(1),
-        )
-        react_strip(1, now)
-        react_plane(0, now)
-        react_plane(9, now)
+            rim_step(step - 1, now)
+            rim_planes(old)
+
+        strip_sums(tiles(old), strips_of(old), move_strip(0))
+        react_strip(0, now)
+
+        @pl.when(step < HOPS)
+        def _():
+            for way in ways:
+                sending(ends_x, way, strip_hop(way, step, now).start)
+
+        edge_sums(tiles(old), strips_of(old), move_plane)
+        react_pair(0, now)
         return carry
 
     lax.fori_loop(1, STEPS, advance, 0)
@@ -683,21 +769,21 @@
     ]
     stores[0].start()
     last = (STEPS - 1) % 2
-    inner_sums(
-        packed_tiles(last),
-        strip_packed[last, 0],
-        strip_packed[last, 1],
-        range(INNER),
-        move_plane,
-        None,
-    )
+    inner_sums(tiles(last), strips_of(last), move_plane)
+    for way in ways:
+        for copy in (hop(way, HOPS - 1, 1 - last), strip_hop(way, HOPS - 1, 1 - last)):
+            receiving(ends_x, way, copy.wait_recv)
+    rim_step(STEPS - 1, 1 - last)
+    rim_planes(last)
+    edge_sums(tiles(last), strips_of(last), move_plane)
     stores[1].start()
-    for copies in (early, lead, late, bulk, pass_on, pass_gates):
-        for copy in copies:
-            copy.wait_send()
-    for way in range(2):
-        for step in (HOPS - 2, HOPS - 1):
-            hop(way, step).wait_send()
+    for way in ways:
+        for copy in (hop(way, HOPS - 1, 1 - last), strip_hop(way, HOPS - 1, 1 - last)):
+            sending(ends_x, way, copy.wait_send)
+        sending(ends_y, way, early[way].wait_send)
+        sending(ends_y, way, late[way].wait_send)
+        sending(ends_x, way, relay[way].wait_send)
+        sending(ends_x, way, relay_gates[way].wait_send)
     for copy in stores:
         copy.wait()
 
@@ -724,12 +810,12 @@
             vmem((2, 2, 16, 128), f32),
             vmem((2, 16, 128), f32),
             vmem((2, 16, 128), f32),
+            vmem((16, 128), f32),
             vmem((9, 16, 128), f32),
-            vmem((2, 2, 16, 384), f32),
-            vmem((2, HOPS, 16, 384), f32),
-            vmem((2, 16, 640), f32),
-            vmem((2, 16, 640), f32),
-            vmem((2, 11, 16, 256), f32),
+            vmem((2, HOPS, 16, 256), f32),
+            vmem((2, HOPS, 16, 128), f32),
+            vmem((16, 128), f32),
+            vmem((2, 16, 128), f32),
             vmem((13, 16, 128), f32),
             vmem((2, 13, 16, 128), f32),
             vmem((2, 16, 128), f32),
@@ -738,10 +824,10 @@
             vmem((2, 16, 256), f32),
             sems((2, HOPS)),
             sems((2, HOPS)),
-            sems((2,)),
-            sems((2,)),
-            sems((2,)),
-            sems((2,)),
+            sems((2, HOPS)),
+            sems((2, HOPS)),
+            sems((5, 2)),
+            sems((5, 2)),
             sems((2, 2)),
             sems((2, 2)),
             sems((2, 2)),
@@ -751,7 +837,7 @@
         ],
         compiler_params=pltpu.CompilerParams(collective_id=0, has_side_effects=True),
         name="slab",
-    )(state, tissue_mask, layer_index, fibre)
+    )(state, jnp.swapaxes(tissue_mask, 1, 2), layer_index, fibre)
 
 
 def solution(mesh):

time: 49.9 us -> 41.9 us (0.84)
  the two profiles are of different devices: /device:TPU:6 before, /device:TPU:91 now
where the time goes in v2:
time: 41.9 us; the launch traced here: 41.8 us
  Pallas kernels  39.1 us (93%)
  local copies, waits for them, and re-layouts  2.67 us (6%)
    pallas_call x1, Pallas kernels, shards(): pl.pallas_call(kernel, out_shape=jax.ShapeDtypeStruct(state.shape, f32),...  39.1 us
    unnamed x1, local copies, waits for them, and re-layouts  2.67 us

profile of v2, /device:TPU:91, one launch (start us, length us, event | category | flops | bytes accessed | tf_op | source)
XLA Modules:
  0.0 41.8 jit_solution(173582693098403149)
XLA Ops:
  0.0 39.1 %slab.1 = f32[12,8,16,256]{3,2,1,0:T(8,128)} custom-call(f32[12,8,16,256]{3,2,1,0:T(8,128)} %state_ref.1, s32[8,2,16]{2,1,0:T(2,128)} %bitcast.1, s32[16]{0:T(128)} %layer_ref.1, f32[2,8]{1,0:T(2,128)} %fibre_ref.1), custom_call_target="tpu_custom_call" | custom-call | tf_op jit(solution)/shard_map/slab/pallas_call | solution.py:794
  39.1 2.7 %copy.6 = f32[12,8,16,256]{3,2,1,0:T(8,128)} copy(f32[12,8,16,256]{3,2,1,0:T(8,128)} %slab.1) | data formatting | bytes 3145728

commit v3 on v2

v3 whole, which is shorter than its diff:
```python
import math

import jax
import jax.numpy as jnp
from jax import lax
from jax.experimental import pallas as pl
from jax.experimental.pallas import tpu as pltpu
from jax.sharding import PartitionSpec as P

STEPS = 8
TRANSVERSE = 0.04
LONGITUDINAL = 0.12
DT = 0.02
RTF = 8314.472 * 310.0 / 96485.3415
EK = RTF * math.log(5.4 / 138.3)
ENA = RTF * math.log(140.0 / 7.67)
EKS = RTF * math.log((5.4 + 0.03 * 140.0) / (138.3 + 0.03 * 7.67))
L2E = 1.0 / math.log(2.0)
KAPPA = -DT * L2E


def grow(volt, slope):
    return jnp.exp2(volt * (slope * L2E))


def sig(volt, centre, width):
    return jax.nn.sigmoid(volt * (1.0 / width) + (-centre / width))


def settle(gate, steady, factor):
    return steady + (gate - steady) * jnp.exp2(factor)


def membrane(s):
    x, m, h, j, d, f, r, z, p, q, w, ca = s
    v = x * 100.0
    over = v - EK
    b = grow(v, 0.05)
    ib = 1.0 / b
    b2 = b * b
    ib2 = ib * ib
    c = jnp.maximum(ca, 0.02)
    vca = (v - 0.5 * RTF * math.log(2000.0)) + (0.5 * RTF) * jnp.log(c)
    sodium = ((14.838 * m) * (m * m) * (h * j) + 0.00029) * (v - ENA)
    calcium = (0.08 * d * f + 0.000592) * vca
    sa = sig(v, EK + 200.0, -1.0 / 0.06)
    bk = (
        (30.0 * math.exp(0.0002 * (100.0 - EK))) * grow(v, 0.0002)
        + (10.0 * math.exp(0.1 * (-EK - 10.0))) * b2
    ) * sig(v, EK, 2.0)
    inward = 5.405 * sa / (sa + bk)
    potassium = (
        0.294 * r * z + 0.153 * p * q + inward + 0.0146 * sig(v, 25.0, 5.98)
    ) * over
    slow = (0.392 * w) * w * (v - EKS)
    en = grow(v, -1.0 / RTF)
    pump = (2.724 * 5.4 / 6.4 * 7.67 / 47.67) / (
        1.0 + 0.1245 * grow(v, -0.1 / RTF) + 0.0353 * en
    )
    ef = grow(v, 0.35 / RTF)
    eg = ef * en
    scale = 1000.0 / ((87.5**3 + 140.0**3) * 3.38)
    exchange = (
        (scale * 7.67**3 * 2.0) * ef - (scale * 2.5 * 140.0**3 * 0.001) * eg * c
    ) / (1.0 + 0.1 * eg)
    pump_ca = 0.1238 * c / (c + 0.5)
    total = sodium + calcium + potassium + slow + pump + exchange + pump_ca
    nx = x - (DT / 100.0) * total
    nca = ca - (DT * 0.05) * (calcium + pump_ca - 2.0 * exchange)
    low = 1.0 / (1.0 + math.exp(20.0) * grow(v, 0.5))
    nm = settle(
        m,
        sig(v, -56.86, 9.03) ** 2,
        (10.0 * KAPPA + (10.0 * KAPPA * math.exp(-12.0)) * (ib2 * ib2))
        / (sig(v, -35.0, -5.0) + sig(v, 50.0, -200.0)),
    )
    hs = sig(v, -71.55, -7.43)
    hs = hs * hs
    up = (KAPPA * 0.77 / 0.13) * sig(v, -10.66, 11.1)
    dn = (
        (KAPPA * 0.057 * math.exp(-80.0 / 6.8)) * grow(v, -1.0 / 6.8)
        + (KAPPA * 2.7) * grow(v, 0.079)
        + (KAPPA * 310000.0) * grow(v, 0.3485)
    )
    nh = settle(h, hs, up + low * (dn - up))
    up = (KAPPA * 0.6) * grow(v, 0.057) * sig(v, -32.0, 10.0)
    dn = ((KAPPA * -25428.0) * grow(v, 0.2444) - (KAPPA * 6.948e-06) * grow(v, -0.04391)) * (
        v + 37.78
    ) * sig(v, -79.23, -1.0 / 0.311) + (KAPPA * 0.02424) * grow(v, -0.01052) * sig(
        v, -40.14, 1.0 / 0.1378
    )
    nj = settle(j, hs, up + low * (dn - up))
    nd = settle(
        d,
        sig(v, -8.0, 7.5),
        KAPPA
        / ((1.96 * sig(v, -35.0, 13.0) + 0.35) * sig(v, -5.0, -5.0) + sig(v, 50.0, 20.0)),
    )
    t = v + 27.0
    nf = settle(
        f,
        sig(v, -20.0, -7.0),
        1.0
        / (
            (1102.5 / KAPPA) * jnp.exp2(t * t * (-L2E / 225.0))
            + (200.0 / KAPPA) * sig(v, 13.0, 10.0)
            + (180.0 / KAPPA) * sig(v, -30.0, -10.0)
            + 20.0 / KAPPA
        ),
    )
    t = v + 40.0
    nr = settle(
        r,
        sig(v, 20.0, 6.0),
        1.0 / ((9.5 / KAPPA) * jnp.exp2(t * t * (-L2E / 1800.0)) + 0.8 / KAPPA),
    )
    t = v + 45.0
    nz = settle(
        z,
        sig(v, -20.0, -5.0),
        1.0
        / (
            (85.0 / KAPPA) * jnp.exp2(t * t * (-L2E / 320.0))
            + (5.0 / KAPPA) * sig(v, 20.0, -5.0)
            + 3.0 / KAPPA
        ),
    )
    k = KAPPA / 2700.0
    np_ = settle(
        p,
        sig(v, -26.0, 7.0),
        (k + (k * math.exp(-4.5)) * ib2)
        * (1.0 + math.exp(30.0 / 11.5) * grow(v, 1.0 / 11.5)),
    )
    k = KAPPA / 3.36
    nq = settle(
        q,
        sig(v, -88.0, -24.0),
        (k * (1.0 + math.exp(-6.0))) + (k * math.exp(-3.0)) * (b + ib),
    )
    nw = settle(
        w,
        sig(v, -5.0, 14.0),
        1.0
        / (
            lax.rsqrt(1.0 + math.exp(5.0 / 6.0) * grow(v, -1.0 / 6.0))
            * ((1400.0 / KAPPA) * sig(v, 35.0, -15.0))
            + 80.0 / KAPPA
        ),
    )
    return nx, nm, nh, nj, nd, nf, nr, nz, np_, nq, nw, nca


INNER = 8
COMPS = 12
HOPS = STEPS - 1
MESH = pl.DeviceIdType.MESH


def react(state, inside):
    fresh = membrane(state)
    return [jnp.where(inside, new, old) for new, old in zip(fresh, state)]


def lanes():
    return lax.broadcasted_iota(jnp.int32, (16, 128), 1)


def turn(tile, shift):
    shift = shift % 128
    return tile if shift == 0 else pltpu.roll(tile, shift, 1)


def coefficients(layer_ref, fibre_ref, coef):
    row = lax.broadcasted_iota(jnp.int32, (16, 128), 0)
    angle_in = jnp.zeros((16, 128), jnp.float32)
    angle_out = jnp.zeros((16, 128), jnp.float32)
    for level in range(16):
        layer = layer_ref[level]
        angle_in = jnp.where(row == level, fibre_ref[0, layer], angle_in)
        angle_out = jnp.where(row == level, fibre_ref[1, layer], angle_out)
    along_x = jnp.cos(angle_in) * jnp.cos(angle_out)
    along_y = jnp.sin(angle_in) * jnp.cos(angle_out)
    along_z = jnp.sin(angle_out)
    spread = LONGITUDINAL - TRANSVERSE
    coef[0] = TRANSVERSE + spread * along_x * along_x
    coef[1] = TRANSVERSE + spread * along_y * along_y
    coef[2] = spread * along_x * along_y / 2.0
    parts = (
        TRANSVERSE + spread * along_z * along_z,
        spread * along_x * along_z / 2.0,
        spread * along_y * along_z / 2.0,
    )
    for index, part in enumerate(parts):
        below = (part + pltpu.roll(part, 1, 0)) / 2.0
        above = (part + pltpu.roll(part, 15, 0)) / 2.0
        coef[3 + index] = jnp.where(row == 0, 0.0, below)
        coef[6 + index] = jnp.where(row == 15, 0.0, above)


def lift(tile):
    return pltpu.roll(tile, 15, 0)


def sink(tile):
    return pltpu.roll(tile, 1, 0)


def terms(coef, value, above, below):
    across = above - below
    flat = coef[1] * value
    tilt = coef[2] * across + lift(coef[5] * value) - sink(coef[8] * value)
    rest = (
        coef[0] * (above + below)
        + lift(coef[3] * value + coef[4] * across)
        + sink(coef[6] * value - coef[7] * across)
    )
    return rest, flat + tilt, flat - tilt


def plane_totals(coef, here, above, below, parts, base):
    lane = lanes()
    first, second = (terms(coef, *tiles) for tiles in zip(here, above, below))
    after_first, after_second = pltpu.roll(first[1], 127, 1), pltpu.roll(second[1], 127, 1)
    before_first, before_second = pltpu.roll(first[2], 1, 1), pltpu.roll(second[2], 1, 1)
    enter_low, enter_high = turn(parts[2], -(base + 7)), turn(parts[1], 127 - (base + 8))
    low, high = lane == 0, lane == 127
    totals = (
        first[0]
        + jnp.where(high, after_second, after_first)
        + jnp.where(low, enter_low, before_first),
        second[0]
        + jnp.where(high, enter_high, after_second)
        + jnp.where(low, before_first, before_second),
    )
    return totals, turn(first[1], base + 7), turn(second[2], base + 9)


def strip_total(parts, border):
    column = lax.rem(lanes(), 16)
    after = jnp.where(column == 7, border[0], pltpu.roll(parts[1], 127, 1))
    before = jnp.where(column == 8, border[1], pltpu.roll(parts[2], 1, 1))
    return parts[0] + after + before


def kernel(
    state_ref,
    mask_ref,
    layer_ref,
    fibre_ref,
    cells,
    packed,
    keep,
    mask,
    strip_cells,
    strip_packed,
    strip_keep,
    strip_mask,
    far_mask,
    borders,
    coef,
    hop_in,
    hop_strip_in,
    strip_out,
    spread_out,
    spread_in,
    side_out,
    side_in,
    relay_out,
    relay_in,
    relay_gates_out,
    relay_gates_in,
    hop_send,
    hop_recv,
    strip_send,
    strip_recv,
    lead_send,
    lead_recv,
    side_send,
    side_recv,
    relay_send,
    relay_recv,
    load_sem,
):
    me_x, me_y = lax.axis_index("gx"), lax.axis_index("gy")
    size_x, size_y = lax.axis_size("gx"), lax.axis_size("gy")
    along_x = ((me_x + 1, me_y), (me_x - 1, me_y))
    along_y = ((me_x, me_y + 1), (me_x, me_y - 1))
    ends_x = (me_x < size_x - 1, me_x > 0)
    ends_y = (me_y < size_y - 1, me_y > 0)
    ways = (0, 1)

    def sending(ends, way, action):
        pl.when(ends[way])(action)

    def receiving(ends, way, action):
        pl.when(ends[1 - way])(action)

    barrier = pltpu.get_barrier_semaphore()
    for ends, targets in ((ends_x, along_x), (ends_y, along_y)):
        for way in ways:

            def greet(target=targets[way]):
                pl.semaphore_signal(barrier, inc=1, device_id=target, device_id_type=MESH)

            sending(ends, way, greet)

    corners = [(way_x, way_y) for way_x in ways for way_y in ways]

    def diagonal(way_x, way_y):
        return along_x[way_x][0], along_y[way_y][1]

    for way_x, way_y in corners:

        @pl.when(ends_x[way_x] & ends_y[way_y])
        def _(target=diagonal(way_x, way_y)):
            pl.semaphore_signal(barrier, inc=1, device_id=target, device_id_type=MESH)

    def remote(source, target, sends, recvs, device):
        return pltpu.make_async_remote_copy(
            src_ref=source,
            dst_ref=target,
            send_sem=sends,
            recv_sem=recvs,
            device_id=device,
            device_id_type=MESH,
        )

    def load(plane):
        return pltpu.make_async_copy(
            state_ref.at[:, plane], cells.at[:, plane + 1], load_sem.at[plane]
        )

    for plane in (0, 7, 1, 6, 2, 5, 3, 4):
        load(plane).start()

    lane = lanes()
    coefficients(layer_ref, fibre_ref, coef)
    spread_tile = jnp.zeros((16, 128), jnp.float32)
    unit = (
        lax.broadcasted_iota(jnp.int32, (16, 16), 0) == lax.broadcasted_iota(jnp.int32, (16, 16), 1)
    ).astype(jnp.float32)
    for plane in range(INNER):
        blocks = lax.dot_general(
            unit,
            (mask_ref[plane] > 0).astype(jnp.float32),
            (((1,), (1,)), ((), ())),
            preferred_element_type=jnp.float32,
        )
        for half in range(2):
            tile = jnp.broadcast_to(blocks[:, half : half + 1], (16, 128))
            mask[plane + 2, :, half * 128 : half * 128 + 128] = tile
            spread_tile = jnp.where(lane == 2 * plane + half, tile, spread_tile)
    spread_out[...] = spread_tile

    for way in ways:

        @pl.when(jnp.logical_not(ends_x[1 - way]))
        def _(way=way):
            for step in range(HOPS):
                hop_in[way, step] = jnp.zeros((16, 256), jnp.float32)
                hop_strip_in[way, step] = jnp.zeros((16, 128), jnp.float32)
            spread_in[way] = jnp.zeros((16, 128), jnp.float32)
            for comp in range(COMPS):
                cells[comp, 0 if way == 0 else 9] = jnp.zeros((16, 256), jnp.float32)

        @pl.when(jnp.logical_not(ends_y[1 - way]))
        def _(way=way):
            for index in range(7):
                side_in[way, index] = jnp.zeros((16, 128), jnp.float32)

    for way_x, way_y in corners:

        @pl.when(jnp.logical_not(ends_x[1 - way_x] & ends_y[1 - way_y]))
        def _(slot=(way_x, way_y)):
            relay_in[slot] = jnp.zeros((16, 128), jnp.float32)
            relay_gates_in[slot] = jnp.zeros((16, 256), jnp.float32)

    def react_plane(slot, parity):
        for top in (0, 8):
            rows = pl.ds(top, 8)
            inside = mask[slot + 1, rows] > 0.0
            fresh = react([cells[comp, slot, rows] for comp in range(COMPS)], inside)
            for comp in range(COMPS):
                cells[comp, slot, rows] = fresh[comp]
            packed[parity, slot + 1, rows] = jnp.where(inside, fresh[0], 0.0)

    body = (lane >= 16) & (lane < 112)
    tips = jnp.logical_not(body)
    every = lane >= 0

    def react_strip(which, parity, region):
        for top in (0, 8):
            rows = pl.ds(top, 8)
            inside = strip_mask[which, rows] > 0.0
            fresh = react(
                [strip_cells[which, comp, rows] for comp in range(COMPS)], inside & region[0:8]
            )
            for comp in range(COMPS):
                strip_cells[which, comp, rows] = fresh[comp]
            strip_packed[parity, which, rows] = jnp.where(
                region[0:8], jnp.where(inside, fresh[0], 0.0), strip_packed[parity, which, rows]
            )

    def react_pair(pair, parity):
        react_plane(pair + 1, parity)
        react_plane(8 - pair, parity)

    def first_pair(pair, carry):
        load(pair).wait()
        load(7 - pair).wait()
        react_pair(pair, 0)
        return carry

    lax.fori_loop(0, 4, first_pair, 0)

    inner_half = lax.rem(lane, 16) < 8

    def pack_side(read):
        tile = jnp.zeros((16, 128), jnp.float32)
        for plane in range(INNER):
            first, second = read(plane)
            base = plane * 16
            both = turn(jnp.where(lane < 64, first, second), base + 8)
            tile = jnp.where((lane >= base) & (lane < base + 16), both, tile)
        return tile

    def own(comp):
        return lambda plane: (cells[comp, plane + 1, :, 0:128], cells[comp, plane + 1, :, 128:256])

    own_mask = pack_side(lambda plane: (mask[plane + 2, :, 0:128], mask[plane + 2, :, 128:256]))
    sides = [pack_side(own(0)), own_mask] + [pack_side(own(comp)) for comp in range(1, COMPS)]
    for index in range(7):
        even = sides[2 * index]
        odd = sides[2 * index + 1] if index < 6 else even
        side_out[0, index] = jnp.where(inner_half, even, turn(odd, 8))
        side_out[1, index] = jnp.where(inner_half, turn(odd, -8), even)
    for way, (edge, inward) in enumerate(((7, 6), (0, 1))):
        tile = jnp.zeros((16, 128), jnp.float32)
        parts = (
            (sides[0], edge),
            (own_mask, edge),
            (own_mask, inward),
            (sides[0] * own_mask, inward),
        )
        for group, (part, plane) in enumerate(parts):
            here = (lane >= group * 16) & (lane < group * 16 + 16)
            tile = jnp.where(here, turn(part, group * 16 - plane * 16), tile)
        relay_out[way] = tile
        for half, gates in enumerate((range(1, 9), range(9, 12))):
            tile = jnp.zeros((16, 128), jnp.float32)
            for group, comp in enumerate(gates):
                here = (lane >= group * 16) & (lane < group * 16 + 16)
                tile = jnp.where(here, turn(sides[comp + 1], group * 16 - edge * 16), tile)
            relay_gates_out[way, :, half * 128 : half * 128 + 128] = tile

    peers_x = sum(end.astype(jnp.int32) for end in ends_x)
    peers_y = sum(end.astype(jnp.int32) for end in ends_y)
    peers = peers_x + peers_y + peers_x * peers_y
    pl.semaphore_wait(barrier, peers)

    early, late, lead, bulk = [], [], [], []
    for way, (edge, inward, slot) in enumerate(((7, 6, 0), (0, 1, 9))):
        early.append(
            remote(
                side_out.at[way, 0],
                side_in.at[way, 0],
                side_send.at[0, way],
                side_recv.at[0, way],
                along_y[way],
            )
        )
        late.append(
            remote(
                side_out.at[way, pl.ds(1, 6)],
                side_in.at[way, pl.ds(1, 6)],
                side_send.at[1, way],
                side_recv.at[1, way],
                along_y[way],
            )
        )
        lead.append(
            [
                remote(
                    source, target, lead_send.at[index, way], lead_recv.at[index, way], along_x[way]
                )
                for index, (source, target) in enumerate(
                    (
                        (cells.at[0, edge + 1], cells.at[0, slot]),
                        (packed.at[0, inward + 2], hop_in.at[way, 0]),
                        (spread_out, spread_in.at[way]),
                    )
                )
            ]
        )
        bulk.append(
            [
                remote(
                    cells.at[pl.ds(start, size), edge + 1],
                    cells.at[pl.ds(start, size), slot],
                    lead_send.at[index, way],
                    lead_recv.at[index, way],
                    along_x[way],
                )
                for index, start, size in ((3, 1, 11),)
            ]
        )
    def corner_copy(way_x, way_y, index):
        source, target = ((relay_out, relay_in), (relay_gates_out, relay_gates_in))[index]
        return remote(
            source.at[way_x],
            target.at[way_x, way_y],
            relay_send.at[index, way_x, way_y],
            relay_recv.at[index, way_x, way_y],
            diagonal(way_x, way_y),
        )

    def corner_start(index):
        for way_x, way_y in corners:

            @pl.when(ends_x[way_x] & ends_y[way_y])
            def _(way_x=way_x, way_y=way_y):
                corner_copy(way_x, way_y, index).start()

    def corner_sent(index):
        for way_x, way_y in corners:

            @pl.when(ends_x[way_x] & ends_y[way_y])
            def _(way_x=way_x, way_y=way_y):
                corner_copy(way_x, way_y, index).wait_send()

    def corner_wait(index):
        for way_x, way_y in corners:

            @pl.when(ends_x[1 - way_x] & ends_y[1 - way_y])
            def _(way_x=way_x, way_y=way_y):
                corner_copy(way_x, way_y, index).wait_recv()

    corner_start(0)
    for way in ways:
        sending(ends_y, way, early[way].start)
    for way in ways:
        for copy in lead[way]:
            sending(ends_x, way, copy.start)
    for way in ways:
        sending(ends_y, way, late[way].start)
    corner_start(1)
    for way in ways:
        for copy in bulk[way]:
            sending(ends_x, way, copy.start)

    def unpack(index):
        even = jnp.where(inner_half, side_in[0, index], side_in[1, index])
        odd = jnp.where(inner_half, turn(side_in[0, index], -8), turn(side_in[1, index], 8))
        return even, odd

    for way in ways:
        receiving(ends_y, way, early[way].wait_recv)
    strip_cells[0, 0], strip_mask[0] = unpack(0)
    strip_packed[0, 0] = strip_mask[0] * strip_cells[0, 0]

    def load_factors():
        return [coef[index] for index in range(9)]

    def sum_planes(factors, read, planes, parts, border, emit):
        leave_low, leave_high = border
        for plane, base, around in planes:
            below, above = around or (read(plane - 1), read(plane + 1))
            totals, low, high = plane_totals(factors, read(plane), above, below, parts, base)
            for half in range(2):
                emit(plane, half, totals[half])
            leave_low = jnp.where(lane == base + 7, low, leave_low)
            leave_high = jnp.where(lane == base + 8, high, leave_high)
        return leave_low, leave_high

    empty = jnp.zeros((16, 128), jnp.float32)

    def inner_sums(read, strip, kept, emit):
        factors = load_factors()
        parts = terms(factors, strip, turn(strip, 112), turn(strip, 16))
        planes = [(plane, 16 * plane, None) for plane in range(2, INNER - 2)]
        border = sum_planes(factors, read, planes, parts, (empty, empty), emit)
        for index, tile in enumerate(border):
            borders[kept, index] = tile

    def middle_sums(read, strip, kept, emit, emit_strip):
        factors = load_factors()
        parts = terms(factors, strip, turn(strip, 112), turn(strip, 16))
        planes = [(plane, 16 * plane, None) for plane in (1, INNER - 2)]
        border = borders[kept, 0], borders[kept, 1]
        border = sum_planes(factors, read, planes, parts, border, emit)
        emit_strip(strip_total(parts, border))

    def edge_sums(read, strips, emit, emit_strip):
        factors = load_factors()
        strip, outer = strips
        above = jnp.where(lane >= 112, turn(outer, 96), turn(strip, 112))
        below = jnp.where(lane < 16, outer, turn(strip, 16))
        parts = terms(factors, strip, above, below)
        planes = [(plane, 16 * plane, None) for plane in (0, INNER - 1)]
        border = sum_planes(factors, read, planes, parts, (empty, empty), emit)
        if emit_strip is not None:
            emit_strip(strip_total(parts, border))

    def rim_sums(read, strips, far, emit, emit_strip):
        factors = load_factors()
        strip, outer = strips
        beyond = empty
        planes = []
        for way, (rim, near) in enumerate(((-1, 0), (INNER, INNER - 1))):
            first, second, far_strip, base = far(way)
            place = way * 16
            here = (lane >= place) & (lane < place + 16)
            beyond = jnp.where(here, turn(far_strip, place - base), beyond)
            pair = ((first, second), read(near))
            planes.append((rim, place, pair if way == 0 else pair[::-1]))
        lower = lane < 16
        near = jnp.where(lower, strip, turn(strip, 32))
        parts = terms(
            factors, outer, jnp.where(lower, near, beyond), jnp.where(lower, beyond, near)
        )
        border = sum_planes(factors, read, planes, parts, (empty, empty), emit)
        emit_strip(strip_total(parts, border))

    def mask_tiles(plane):
        return mask[plane + 2, :, 0:128], mask[plane + 2, :, 128:256]

    def keep_plane(plane, half, total):
        columns = slice(half * 128, half * 128 + 128)
        keep[plane + 1, :, columns] = 1.0 - mask[plane + 2, :, columns] * total

    def keep_strip(which, region):
        def emit(total):
            strip_keep[which] = jnp.where(
                region, 1.0 - strip_mask[which] * total, strip_keep[which]
            )

        return emit

    def mask_far(way):
        return (*mask_tiles(-2 if way == 0 else 9), far_mask[...], way * 16)

    def move_plane(plane, half, total):
        columns = slice(half * 128, half * 128 + 128)
        cells[0, plane + 1, :, columns] = (
            cells[0, plane + 1, :, columns] * keep[plane + 1, :, columns]
            + mask[plane + 2, :, columns] * total
        )

    def move_strip(which, region):
        def emit(total):
            value = strip_cells[which, 0]
            moved = value * strip_keep[which] + strip_mask[which] * total
            strip_cells[which, 0] = jnp.where(region, moved, value)

        return emit

    def tiles(parity):
        return lambda plane: (
            packed[parity, plane + 2, :, 0:128],
            packed[parity, plane + 2, :, 128:256],
        )

    def strips_of(parity):
        return strip_packed[parity, 0], strip_packed[parity, 1]

    def hop(way, step, parity):
        return remote(
            packed.at[parity, 8 if way == 0 else 3],
            hop_in.at[way, step],
            hop_send.at[way, step],
            hop_recv.at[way, step],
            along_x[way],
        )

    def strip_hop(way, step, parity):
        return remote(
            strip_out.at[parity],
            hop_strip_in.at[way, step],
            strip_send.at[way, step],
            strip_recv.at[way, step],
            along_x[way],
        )

    def rim_step(step, parity):
        def far(way):
            return (
                hop_in[way, step - 1, :, 0:128],
                hop_in[way, step - 1, :, 128:256],
                hop_strip_in[way, step - 1],
                96 if way == 0 else 16,
            )

        read, strips = tiles(parity), strips_of(parity)
        rim_sums(read, strips, far, move_plane, move_strip(1, every))

    def rim_planes(parity):
        react_plane(0, parity)
        react_plane(9, parity)

    def open_rim():
        corner_wait(0)
        for way in ways:
            for copy in lead[way]:
                receiving(ends_x, way, copy.wait_recv)
        outer_mask = jnp.zeros((16, 128), jnp.float32)
        outer_far_mask = jnp.zeros((16, 128), jnp.float32)
        outer_first = jnp.zeros((16, 128), jnp.float32)
        for way, (edge, inward, slot, beyond) in enumerate(((7, 6, 1, 0), (0, 1, 10, 11))):
            for half in range(2):
                columns = slice(half * 128, half * 128 + 128)
                for plane, target in ((edge, slot), (inward, beyond)):
                    index = 2 * plane + half
                    mask[target, :, columns] = jnp.broadcast_to(
                        spread_in[way, :, index : index + 1], (16, 128)
                    )
            packed[0, slot] = mask[slot] * cells[0, slot - 1]
            place = way * 16
            here = (lane >= place) & (lane < place + 16)
            relayed = jnp.where(inner_half, relay_in[way, 0], relay_in[way, 1])
            outer_first = jnp.where(here, turn(relayed, place), outer_first)
            outer_mask = jnp.where(here, turn(relayed, place - 16), outer_mask)
            outer_far_mask = jnp.where(here, turn(relayed, place - 32), outer_far_mask)
            hop_strip_in[way, 0] = turn(relayed, inward * 16 - 48)
        strip_cells[1, 0] = outer_first
        strip_mask[1] = outer_mask
        strip_packed[0, 1] = outer_mask * outer_first
        far_mask[...] = outer_far_mask
        masks = (strip_mask[0], outer_mask)
        edge_sums(mask_tiles, masks, keep_plane, keep_strip(0, tips))
        rim_sums(mask_tiles, masks, mask_far, keep_plane, keep_strip(1, every))

    def open_rim_gates():
        corner_wait(1)
        for way in ways:
            for copy in bulk[way]:
                receiving(ends_x, way, copy.wait_recv)
        for half, gates in enumerate((range(1, 9), range(9, 12))):
            for group, comp in enumerate(gates):
                tile = jnp.zeros((16, 128), jnp.float32)
                for way in ways:
                    place = way * 16
                    here = (lane >= place) & (lane < place + 16)
                    columns = slice(half * 128, half * 128 + 128)
                    source = jnp.where(
                        inner_half,
                        relay_gates_in[way, 0, :, columns],
                        relay_gates_in[way, 1, :, columns],
                    )
                    tile = jnp.where(here, turn(source, place - group * 16), tile)
                strip_cells[1, comp] = tile

    def open_strip_gates():
        for way in ways:
            receiving(ends_y, way, late[way].wait_recv)
        for index in range(1, 7):
            even, odd = unpack(index)
            strip_cells[0, 2 * index - 1] = even
            if index < 6:
                strip_cells[0, 2 * index] = odd

    inner_sums(mask_tiles, strip_mask[0], 0, keep_plane)
    middle_sums(mask_tiles, strip_mask[0], 0, keep_plane, keep_strip(0, body))
    inner_sums(tiles(0), strip_packed[0, 0], 1, move_plane)

    def advance(step):
        first, second = (isinstance(step, int) and step == value for value in (1, 2))
        now = lax.rem(step, 2)
        old = 1 - now
        if not (first or second):
            for way in ways:
                sending(ends_x, way, hop(way, step - 2, now).wait_send)
                sending(ends_x, way, strip_hop(way, step - 2, now).wait_send)
        middle_sums(tiles(old), strip_packed[old, 0], 1, move_plane, move_strip(0, body))
        if not second:
            react_pair(3, now)
        if first:
            open_strip_gates()
        react_strip(0, now, body)
        strip_out[now] = strip_packed[now, 0]
        react_pair(1, now)

        @pl.when(step < HOPS)
        def _():
            for way in ways:
                sending(ends_x, way, hop(way, step, now).start)
                sending(ends_x, way, strip_hop(way, step, now).start)

        if first:
            react_pair(2, now)
            inner_sums(tiles(now), strip_packed[now, 0], 1, move_plane)
            react_pair(3, old)
            react_pair(2, old)
            open_rim()
            for way in ways:
                for copy in lead[way] + bulk[way]:
                    sending(ends_x, way, copy.wait_send)
        elif second:
            open_rim_gates()
        else:
            for way in ways:
                for copy in (hop(way, step - 2, now), strip_hop(way, step - 2, now)):
                    receiving(ends_x, way, copy.wait_recv)
        if not first:
            rim_step(step - 1, now)
            if not second:
                react_pair(2, now)
            react_strip(1, old, every)
            rim_planes(old)
        edge_sums(tiles(old), strips_of(old), move_plane, move_strip(0, tips))
        react_strip(0, now, tips)
        if not first:
            inner_sums(tiles(now), strip_packed[now, 0], 1, move_plane)
        react_pair(0, now)

    advance(1)
    advance(2)

    def later(step, carry):
        advance(step)
        return carry

    lax.fori_loop(3, STEPS, later, 0)

    last = (STEPS - 1) % 2
    middle_sums(tiles(last), strip_packed[last, 0], 1, move_plane, lambda total: None)
    for way in ways:
        for copy in (hop(way, HOPS - 1, 1 - last), strip_hop(way, HOPS - 1, 1 - last)):
            receiving(ends_x, way, copy.wait_recv)
    rim_step(STEPS - 1, 1 - last)
    react_strip(1, last, every)
    rim_planes(last)
    edge_sums(tiles(last), strips_of(last), move_plane, None)
    corner_sent(0)
    corner_sent(1)
    for way in ways:
        for copy in (hop(way, HOPS - 1, 1 - last), strip_hop(way, HOPS - 1, 1 - last)):
            sending(ends_x, way, copy.wait_send)
        sending(ends_y, way, early[way].wait_send)
        sending(ends_y, way, late[way].wait_send)


def unload(cells, out_ref, store_sem):
    stores = [
        pltpu.make_async_copy(
            cells.at[comp, pl.ds(1, INNER)], out_ref.at[comp], store_sem.at[comp]
        )
        for comp in range(COMPS)
    ]
    for copy in stores:
        copy.start()
    for copy in stores:
        copy.wait()


def shards(state, tissue_mask, layer_index, fibre):
    vmem, sems = pltpu.VMEM, pltpu.SemaphoreType.DMA
    f32 = jnp.float32
    cells = pl.pallas_call(
        kernel,
        out_shape=vmem((COMPS, 10, 16, 256), f32),
        in_specs=[
            pl.BlockSpec(memory_space=pl.ANY),
            pl.BlockSpec(memory_space=pltpu.VMEM),
            pl.BlockSpec(memory_space=pltpu.SMEM),
            pl.BlockSpec(memory_space=pltpu.SMEM),
        ],
        out_specs=pl.BlockSpec(memory_space=pltpu.VMEM),
        scratch_shapes=[
            vmem((2, 12, 16, 256), f32),
            vmem((10, 16, 256), f32),
            vmem((12, 16, 256), f32),
            vmem((2, COMPS, 16, 128), f32),
            vmem((2, 2, 16, 128), f32),
            vmem((2, 16, 128), f32),
            vmem((2, 16, 128), f32),
            vmem((16, 128), f32),
            vmem((2, 4, 16, 128), f32),
            vmem((9, 16, 128), f32),
            vmem((2, HOPS, 16, 256), f32),
            vmem((2, HOPS, 16, 128), f32),
            vmem((2, 16, 128), f32),
            vmem((16, 128), f32),
            vmem((2, 16, 128), f32),
            vmem((2, 7, 16, 128), f32),
            vmem((2, 7, 16, 128), f32),
            vmem((2, 16, 128), f32),
            vmem((2, 2, 16, 128), f32),
            vmem((2, 16, 256), f32),
            vmem((2, 2, 16, 256), f32),
            sems((2, HOPS)),
            sems((2, HOPS)),
            sems((2, HOPS)),
            sems((2, HOPS)),
            sems((4, 2)),
            sems((4, 2)),
            sems((2, 2)),
            sems((2, 2)),
            sems((2, 2, 2)),
            sems((2, 2, 2)),
            sems((INNER,)),
        ],
        compiler_params=pltpu.CompilerParams(collective_id=0, has_side_effects=True, vmem_limit_bytes=64000000),
        name="slab",
    )(state, jnp.swapaxes(tissue_mask, 1, 2), layer_index, fibre)
    return pl.pallas_call(
        unload,
        out_shape=jax.ShapeDtypeStruct(state.shape, f32),
        in_specs=[pl.BlockSpec(memory_space=pl.ANY)],
        out_specs=pl.BlockSpec(memory_space=pl.ANY),
        scratch_shapes=[sems((COMPS,))],
        compiler_params=pltpu.CompilerParams(vmem_limit_bytes=1 << 20),
        name="unload",
    )(cells)


def solution(mesh):
    placed = (P(None, "gx", None, "gy"), P("gx", None, "gy"), P(), P())
    return jax.shard_map(
        shards, mesh=mesh, in_specs=placed, out_specs=P(None, "gx", None, "gy"), check_vma=False
    )
```

time: 41.9 us -> 37 us (0.88)
  local copies, waits for them, and re-layouts: 2.67 us -> 0 us
  Pallas kernels: 39.1 us -> 36.7 us
    unnamed x1 -> x0, local copies, waits for them, and re-layouts: 2.67 us -> none
    pallas_call x1 -> x2, Pallas kernels: 39.1 us -> 36.7 us  [the longest x1 35.5 us: shards(): pl.pallas_call(kernel, out_shape=vmem((COMPS, 10, 16, 256), f32), in_spec...]
where the time goes in v3:
time: 37 us; the launch traced here: 36.7 us
  Pallas kernels  36.7 us (99%)
    pallas_call x1, Pallas kernels, shards(): pl.pallas_call(kernel, out_shape=vmem((COMPS, 10, 16, 256), f32), in_spec...  35.5 us
    pallas_call x1, Pallas kernels, shards(): pl.pallas_call(unload, out_shape=jax.ShapeDtypeStruct(state.shape, f32),...  1.23 us

profile of v3, /device:TPU:91, one launch (start us, length us, event | category | flops | bytes accessed | tf_op | source)
XLA Modules:
  0.0 36.7 jit_solution(10281136710392595398)
XLA Ops:
  0.0 35.5 %slab.1.cells = f32[12,10,16,256]{3,2,1,0:T(8,128)S(1)} custom-call(f32[12,8,16,256]{3,2,1,0:T(8,128)} %state_ref.1, s32[8,2,16]{2,1,0:T(2,128)} %bitcast.1, s32[16]{0:T(128)} %layer_ref.1, f32[2,8]{1,0:T(2,128)} %fibre_ref.1), custom_call_target="tpu_custom_call" | custom-call | tf_op jit(solution)/shard_map/slab/pallas_call | solution.py:859
  35.5 1.2 %unload.1 = f32[12,8,16,256]{3,2,1,0:T(8,128)} custom-call(f32[12,10,16,256]{3,2,1,0:T(8,128)S(1)} %slab.1.cells), custom_call_target="tpu_custom_call" | custom-call | tf_op jit(solution)/shard_map/unload/pallas_call | solution.py:906

commit v4 on v3

--- a/solution.py
+++ b/solution.py
@@ -218,12 +218,11 @@
     return rest, flat + tilt, flat - tilt
 
 
-def plane_totals(coef, here, above, below, parts, base):
+def plane_totals(coef, here, above, below, enter_low, enter_high):
     lane = lanes()
     first, second = (terms(coef, *tiles) for tiles in zip(here, above, below))
     after_first, after_second = pltpu.roll(first[1], 127, 1), pltpu.roll(second[1], 127, 1)
     before_first, before_second = pltpu.roll(first[2], 1, 1), pltpu.roll(second[2], 1, 1)
-    enter_low, enter_high = turn(parts[2], -(base + 7)), turn(parts[1], 127 - (base + 8))
     low, high = lane == 0, lane == 127
     totals = (
         first[0]
@@ -233,7 +232,7 @@
         + jnp.where(high, enter_high, after_second)
         + jnp.where(low, before_first, before_second),
     )
-    return totals, turn(first[1], base + 7), turn(second[2], base + 9)
+    return totals, first[1], second[2]
 
 
 def strip_total(parts, border):
@@ -256,11 +255,12 @@
     strip_packed,
     strip_keep,
     strip_mask,
-    far_mask,
     borders,
     coef,
     hop_in,
     hop_strip_in,
+    twin_in,
+    twin_strip_in,
     strip_out,
     spread_out,
     spread_in,
@@ -274,6 +274,10 @@
     hop_recv,
     strip_send,
     strip_recv,
+    twin_send,
+    twin_recv,
+    twin_strip_send,
+    twin_strip_recv,
     lead_send,
     lead_recv,
     side_send,
@@ -286,6 +290,11 @@
     size_x, size_y = lax.axis_size("gx"), lax.axis_size("gy")
     along_x = ((me_x + 1, me_y), (me_x - 1, me_y))
     along_y = ((me_x, me_y + 1), (me_x, me_y - 1))
+    odd = lax.rem(me_x, 2)
+    even = odd == 0
+    twin = (me_x + 1 - 2 * odd, me_y)
+    partner = (me_x - 1 + 2 * odd, me_y)
+    has_rim = (even & (me_x > 0)) | (jnp.logical_not(even) & (me_x < size_x - 1))
     ends_x = (me_x < size_x - 1, me_x > 0)
     ends_y = (me_y < size_y - 1, me_y > 0)
     ways = (0, 1)
@@ -353,16 +362,19 @@
             spread_tile = jnp.where(lane == 2 * plane + half, tile, spread_tile)
     spread_out[...] = spread_tile
 
+    @pl.when(jnp.logical_not(has_rim))
+    def _():
+        for step in range(HOPS):
+            hop_in[step] = jnp.zeros((16, 256), jnp.float32)
+            hop_strip_in[step] = jnp.zeros((16, 128), jnp.float32)
+        for comp in range(COMPS):
+            cells[comp, 9 * odd] = jnp.zeros((16, 256), jnp.float32)
+
     for way in ways:
 
         @pl.when(jnp.logical_not(ends_x[1 - way]))
         def _(way=way):
-            for step in range(HOPS):
-                hop_in[way, step] = jnp.zeros((16, 256), jnp.float32)
-                hop_strip_in[way, step] = jnp.zeros((16, 128), jnp.float32)
             spread_in[way] = jnp.zeros((16, 128), jnp.float32)
-            for comp in range(COMPS):
-                cells[comp, 0 if way == 0 else 9] = jnp.zeros((16, 256), jnp.float32)
 
         @pl.when(jnp.logical_not(ends_y[1 - way]))
         def _(way=way):
@@ -431,10 +443,10 @@
     own_mask = pack_side(lambda plane: (mask[plane + 2, :, 0:128], mask[plane + 2, :, 128:256]))
     sides = [pack_side(own(0)), own_mask] + [pack_side(own(comp)) for comp in range(1, COMPS)]
     for index in range(7):
-        even = sides[2 * index]
-        odd = sides[2 * index + 1] if index < 6 else even
-        side_out[0, index] = jnp.where(inner_half, even, turn(odd, 8))
-        side_out[1, index] = jnp.where(inner_half, turn(odd, -8), even)
+        one = sides[2 * index]
+        two = sides[2 * index + 1] if index < 6 else one
+        side_out[0, index] = jnp.where(inner_half, one, turn(two, 8))
+        side_out[1, index] = jnp.where(inner_half, turn(two, -8), one)
     for way, (edge, inward) in enumerate(((7, 6), (0, 1))):
         tile = jnp.zeros((16, 128), jnp.float32)
         parts = (
@@ -459,8 +471,8 @@
     peers = peers_x + peers_y + peers_x * peers_y
     pl.semaphore_wait(barrier, peers)
 
-    early, late, lead, bulk = [], [], [], []
-    for way, (edge, inward, slot) in enumerate(((7, 6, 0), (0, 1, 9))):
+    early, late, lead = [], [], []
+    for way in ways:
         early.append(
             remote(
                 side_out.at[way, 0],
@@ -480,31 +492,46 @@
             )
         )
         lead.append(
-            [
-                remote(
-                    source, target, lead_send.at[index, way], lead_recv.at[index, way], along_x[way]
-                )
-                for index, (source, target) in enumerate(
-                    (
-                        (cells.at[0, edge + 1], cells.at[0, slot]),
-                        (packed.at[0, inward + 2], hop_in.at[way, 0]),
-                        (spread_out, spread_in.at[way]),
-                    )
-                )
-            ]
-        )
-        bulk.append(
-            [
-                remote(
-                    cells.at[pl.ds(start, size), edge + 1],
-                    cells.at[pl.ds(start, size), slot],
-                    lead_send.at[index, way],
-                    lead_recv.at[index, way],
-                    along_x[way],
-                )
-                for index, start, size in ((3, 1, 11),)
-            ]
-        )
+            remote(
+                spread_out,
+                spread_in.at[way],
+                lead_send.at[0, way],
+                lead_recv.at[0, way],
+                along_x[way],
+            )
+        )
+
+    def rim_copy(index):
+        source, target = (
+            (cells.at[0, 1 + 7 * odd], cells.at[0, 9 - 9 * odd]),
+            (packed.at[0, 3 + 5 * odd], hop_in.at[0]),
+            (cells.at[pl.ds(1, 11), 1 + 7 * odd], cells.at[pl.ds(1, 11), 9 - 9 * odd]),
+        )[index]
+        return remote(
+            source, target, lead_send.at[index + 1, 0], lead_recv.at[index + 1, 0], partner
+        )
+
+    def rim_action(action):
+        pl.when(has_rim)(action)
+
+    def twin_hop(step, parity):
+        return remote(
+            packed.at[parity, 9 - 7 * odd],
+            twin_in.at[step],
+            twin_send.at[step],
+            twin_recv.at[step],
+            twin,
+        )
+
+    def twin_strip_hop(step, parity):
+        return remote(
+            strip_packed.at[parity, 0],
+            twin_strip_in.at[step],
+            twin_strip_send.at[step],
+            twin_strip_recv.at[step],
+            twin,
+        )
+
     def corner_copy(way_x, way_y, index):
         source, target = ((relay_out, relay_in), (relay_gates_out, relay_gates_in))[index]
         return remote(
@@ -539,20 +566,20 @@
     corner_start(0)
     for way in ways:
         sending(ends_y, way, early[way].start)
+    rim_action(rim_copy(0).start)
+    rim_action(rim_copy(1).start)
     for way in ways:
-        for copy in lead[way]:
-            sending(ends_x, way, copy.start)
+        sending(ends_x, way, lead[way].start)
+    twin_hop(0, 0).start()
     for way in ways:
         sending(ends_y, way, late[way].start)
     corner_start(1)
-    for way in ways:
-        for copy in bulk[way]:
-            sending(ends_x, way, copy.start)
+    rim_action(rim_copy(2).start)
 
     def unpack(index):
-        even = jnp.where(inner_half, side_in[0, index], side_in[1, index])
-        odd = jnp.where(inner_half, turn(side_in[0, index], -8), turn(side_in[1, index], 8))
-        return even, odd
+        one = jnp.where(inner_half, side_in[0, index], side_in[1, index])
+        two = jnp.where(inner_half, turn(side_in[0, index], -8), turn(side_in[1, index], 8))
+        return one, two
 
     for way in ways:
         receiving(ends_y, way, early[way].wait_recv)
@@ -564,13 +591,20 @@
 
     def sum_planes(factors, read, planes, parts, border, emit):
         leave_low, leave_high = border
-        for plane, base, around in planes:
-            below, above = around or (read(plane - 1), read(plane + 1))
-            totals, low, high = plane_totals(factors, read(plane), above, below, parts, base)
+        for plane in planes:
+            base = 16 * plane
+            totals, low, high = plane_totals(
+                factors,
+                read(plane),
+                read(plane + 1),
+                read(plane - 1),
+                turn(parts[2], -(base + 7)),
+                turn(parts[1], 127 - (base + 8)),
+            )
             for half in range(2):
                 emit(plane, half, totals[half])
-            leave_low = jnp.where(lane == base + 7, low, leave_low)
-            leave_high = jnp.where(lane == base + 8, high, leave_high)
+            leave_low = jnp.where(lane == base + 7, turn(low, base + 7), leave_low)
+            leave_high = jnp.where(lane == base + 8, turn(high, base + 9), leave_high)
         return leave_low, leave_high
 
     empty = jnp.zeros((16, 128), jnp.float32)
@@ -578,7 +612,7 @@
     def inner_sums(read, strip, kept, emit):
         factors = load_factors()
         parts = terms(factors, strip, turn(strip, 112), turn(strip, 16))
-        planes = [(plane, 16 * plane, None) for plane in range(2, INNER - 2)]
+        planes = range(2, INNER - 2)
         border = sum_planes(factors, read, planes, parts, (empty, empty), emit)
         for index, tile in enumerate(border):
             borders[kept, index] = tile
@@ -586,7 +620,7 @@
     def middle_sums(read, strip, kept, emit, emit_strip):
         factors = load_factors()
         parts = terms(factors, strip, turn(strip, 112), turn(strip, 16))
-        planes = [(plane, 16 * plane, None) for plane in (1, INNER - 2)]
+        planes = (1, INNER - 2)
         border = borders[kept, 0], borders[kept, 1]
         border = sum_planes(factors, read, planes, parts, border, emit)
         emit_strip(strip_total(parts, border))
@@ -597,30 +631,38 @@
         above = jnp.where(lane >= 112, turn(outer, 96), turn(strip, 112))
         below = jnp.where(lane < 16, outer, turn(strip, 16))
         parts = terms(factors, strip, above, below)
-        planes = [(plane, 16 * plane, None) for plane in (0, INNER - 1)]
+        planes = (0, INNER - 1)
         border = sum_planes(factors, read, planes, parts, (empty, empty), emit)
         if emit_strip is not None:
             emit_strip(strip_total(parts, border))
 
-    def rim_sums(read, strips, far, emit, emit_strip):
+    def rim_sums(read, strips, far, beyond, emit, emit_strip):
         factors = load_factors()
         strip, outer = strips
-        beyond = empty
-        planes = []
-        for way, (rim, near) in enumerate(((-1, 0), (INNER, INNER - 1))):
-            first, second, far_strip, base = far(way)
-            place = way * 16
-            here = (lane >= place) & (lane < place + 16)
-            beyond = jnp.where(here, turn(far_strip, place - base), beyond)
-            pair = ((first, second), read(near))
-            planes.append((rim, place, pair if way == 0 else pair[::-1]))
         lower = lane < 16
-        near = jnp.where(lower, strip, turn(strip, 32))
+        near_strip = jnp.where(lower, strip, turn(strip, 32))
         parts = terms(
-            factors, outer, jnp.where(lower, near, beyond), jnp.where(lower, beyond, near)
-        )
-        border = sum_planes(factors, read, planes, parts, (empty, empty), emit)
-        emit_strip(strip_total(parts, border))
+            factors,
+            outer,
+            jnp.where(lower, near_strip, beyond),
+            jnp.where(lower, beyond, near_strip),
+        )
+        near = read(7 * odd)
+        above = [jnp.where(even, a, b) for a, b in zip(near, far)]
+        below = [jnp.where(even, b, a) for a, b in zip(near, far)]
+        totals, low, high = plane_totals(
+            factors,
+            read(9 * odd - 1),
+            above,
+            below,
+            jnp.where(even, turn(parts[2], -7), turn(parts[2], -23)),
+            jnp.where(even, turn(parts[1], 119), turn(parts[1], 103)),
+        )
+        for half in range(2):
+            emit(9 * odd - 1, half, totals[half])
+        leave_low = jnp.where(lane == 7, turn(low, 7), turn(low, 23))
+        leave_high = jnp.where(lane == 8, turn(high, 9), turn(high, 25))
+        emit_strip(strip_total(parts, (leave_low, leave_high)))
 
     def mask_tiles(plane):
         return mask[plane + 2, :, 0:128], mask[plane + 2, :, 128:256]
@@ -637,9 +679,6 @@
 
         return emit
 
-    def mask_far(way):
-        return (*mask_tiles(-2 if way == 0 else 9), far_mask[...], way * 16)
-
     def move_plane(plane, half, total):
         columns = slice(half * 128, half * 128 + 128)
         cells[0, plane + 1, :, columns] = (
@@ -664,45 +703,51 @@
     def strips_of(parity):
         return strip_packed[parity, 0], strip_packed[parity, 1]
 
-    def hop(way, step, parity):
+    def hop(step, parity):
         return remote(
-            packed.at[parity, 8 if way == 0 else 3],
-            hop_in.at[way, step],
-            hop_send.at[way, step],
-            hop_recv.at[way, step],
-            along_x[way],
-        )
-
-    def strip_hop(way, step, parity):
+            packed.at[parity, 3 + 5 * odd],
+            hop_in.at[step],
+            hop_send.at[step],
+            hop_recv.at[step],
+            partner,
+        )
+
+    def strip_hop(step, parity):
         return remote(
             strip_out.at[parity],
-            hop_strip_in.at[way, step],
-            strip_send.at[way, step],
-            strip_recv.at[way, step],
-            along_x[way],
-        )
+            hop_strip_in.at[step],
+            strip_send.at[step],
+            strip_recv.at[step],
+            partner,
+        )
+
+    rim_lanes = (lane >= 16 * odd) & (lane < 16 * odd + 16)
+    twin_lanes = (lane >= 16 - 16 * odd) & (lane < 32 - 16 * odd)
 
     def rim_step(step, parity):
-        def far(way):
-            return (
-                hop_in[way, step - 1, :, 0:128],
-                hop_in[way, step - 1, :, 128:256],
-                hop_strip_in[way, step - 1],
-                96 if way == 0 else 16,
-            )
-
-        read, strips = tiles(parity), strips_of(parity)
-        rim_sums(read, strips, far, move_plane, move_strip(1, every))
-
-    def rim_planes(parity):
-        react_plane(0, parity)
-        react_plane(9, parity)
+        far = hop_in[step - 1, :, 0:128], hop_in[step - 1, :, 128:256]
+        strip = hop_strip_in[step - 1]
+        beyond = jnp.where(even, turn(strip, 32), strip)
+        rim_sums(
+            tiles(parity), strips_of(parity), far, beyond, move_plane, move_strip(1, rim_lanes)
+        )
+
+    def take_twin(step, parity):
+        twin_hop(step, parity).wait_recv()
+        twin_strip_hop(step, parity).wait_recv()
+        packed[parity, 10 - 9 * odd] = twin_in[step]
+        strip_packed[parity, 1] = jnp.where(
+            twin_lanes, turn(twin_strip_in[step], 16), strip_packed[parity, 1]
+        )
 
     def open_rim():
         corner_wait(0)
         for way in ways:
-            for copy in lead[way]:
-                receiving(ends_x, way, copy.wait_recv)
+            receiving(ends_x, way, lead[way].wait_recv)
+        rim_action(rim_copy(0).wait_recv)
+        rim_action(rim_copy(1).wait_recv)
+        twin_hop(0, 0).wait_recv()
+        moved = []
         outer_mask = jnp.zeros((16, 128), jnp.float32)
         outer_far_mask = jnp.zeros((16, 128), jnp.float32)
         outer_first = jnp.zeros((16, 128), jnp.float32)
@@ -714,27 +759,29 @@
                     mask[target, :, columns] = jnp.broadcast_to(
                         spread_in[way, :, index : index + 1], (16, 128)
                     )
-            packed[0, slot] = mask[slot] * cells[0, slot - 1]
             place = way * 16
             here = (lane >= place) & (lane < place + 16)
             relayed = jnp.where(inner_half, relay_in[way, 0], relay_in[way, 1])
             outer_first = jnp.where(here, turn(relayed, place), outer_first)
             outer_mask = jnp.where(here, turn(relayed, place - 16), outer_mask)
             outer_far_mask = jnp.where(here, turn(relayed, place - 32), outer_far_mask)
-            hop_strip_in[way, 0] = turn(relayed, inward * 16 - 48)
+            moved.append(turn(relayed, inward * 16 - 48))
+        rim_slot = 9 * odd
+        packed[0, rim_slot + 1] = mask[rim_slot + 1] * cells[0, rim_slot]
+        packed[0, 10 - rim_slot] = twin_in[0]
+        hop_strip_in[0] = jnp.where(even, moved[0], moved[1])
         strip_cells[1, 0] = outer_first
         strip_mask[1] = outer_mask
         strip_packed[0, 1] = outer_mask * outer_first
-        far_mask[...] = outer_far_mask
+        strip_packed[1, 1] = empty
         masks = (strip_mask[0], outer_mask)
         edge_sums(mask_tiles, masks, keep_plane, keep_strip(0, tips))
-        rim_sums(mask_tiles, masks, mask_far, keep_plane, keep_strip(1, every))
+        far = mask[11 * odd, :, 0:128], mask[11 * odd, :, 128:256]
+        rim_sums(mask_tiles, masks, far, outer_far_mask, keep_plane, keep_strip(1, every))
 
     def open_rim_gates():
         corner_wait(1)
-        for way in ways:
-            for copy in bulk[way]:
-                receiving(ends_x, way, copy.wait_recv)
+        rim_action(rim_copy(2).wait_recv)
         for half, gates in enumerate((range(1, 9), range(9, 12))):
             for group, comp in enumerate(gates):
                 tile = jnp.zeros((16, 128), jnp.float32)
@@ -754,25 +801,27 @@
         for way in ways:
             receiving(ends_y, way, late[way].wait_recv)
         for index in range(1, 7):
-            even, odd = unpack(index)
-            strip_cells[0, 2 * index - 1] = even
+            one, two = unpack(index)
+            strip_cells[0, 2 * index - 1] = one
             if index < 6:
-                strip_cells[0, 2 * index] = odd
+                strip_cells[0, 2 * index] = two
 
     inner_sums(mask_tiles, strip_mask[0], 0, keep_plane)
     middle_sums(mask_tiles, strip_mask[0], 0, keep_plane, keep_strip(0, body))
     inner_sums(tiles(0), strip_packed[0, 0], 1, move_plane)
 
     def advance(step):
-        first, second = (isinstance(step, int) and step == value for value in (1, 2))
+        first, second, third = (isinstance(step, int) and step == value for value in (1, 2, 3))
+        ahead, done = first or second, second or third
         now = lax.rem(step, 2)
         old = 1 - now
         if not (first or second):
-            for way in ways:
-                sending(ends_x, way, hop(way, step - 2, now).wait_send)
-                sending(ends_x, way, strip_hop(way, step - 2, now).wait_send)
+            rim_action(hop(step - 2, now).wait_send)
+            rim_action(strip_hop(step - 2, now).wait_send)
+            twin_hop(step - 2, now).wait_send()
+            twin_strip_hop(step - 2, now).wait_send()
         middle_sums(tiles(old), strip_packed[old, 0], 1, move_plane, move_strip(0, body))
-        if not second:
+        if not done:
             react_pair(3, now)
         if first:
             open_strip_gates()
@@ -780,62 +829,71 @@
         strip_out[now] = strip_packed[now, 0]
         react_pair(1, now)
 
-        @pl.when(step < HOPS)
+        @pl.when((step < HOPS) & has_rim)
         def _():
-            for way in ways:
-                sending(ends_x, way, hop(way, step, now).start)
-                sending(ends_x, way, strip_hop(way, step, now).start)
+            hop(step, now).start()
+            strip_hop(step, now).start()
 
         if first:
             react_pair(2, now)
+        if ahead:
             inner_sums(tiles(now), strip_packed[now, 0], 1, move_plane)
             react_pair(3, old)
             react_pair(2, old)
+        if first:
             open_rim()
             for way in ways:
-                for copy in lead[way] + bulk[way]:
-                    sending(ends_x, way, copy.wait_send)
+                sending(ends_x, way, lead[way].wait_send)
+            for index in range(3):
+                rim_action(rim_copy(index).wait_send)
+            twin_hop(0, old).wait_send()
         elif second:
             open_rim_gates()
         else:
-            for way in ways:
-                for copy in (hop(way, step - 2, now), strip_hop(way, step - 2, now)):
-                    receiving(ends_x, way, copy.wait_recv)
+            rim_action(hop(step - 2, now).wait_recv)
+            rim_action(strip_hop(step - 2, now).wait_recv)
         if not first:
             rim_step(step - 1, now)
-            if not second:
+            if not done:
                 react_pair(2, now)
-            react_strip(1, old, every)
-            rim_planes(old)
+            react_strip(1, old, rim_lanes)
+            react_plane(9 * odd, old)
+            take_twin(step - 1, old)
         edge_sums(tiles(old), strips_of(old), move_plane, move_strip(0, tips))
         react_strip(0, now, tips)
-        if not first:
+        if not ahead:
             inner_sums(tiles(now), strip_packed[now, 0], 1, move_plane)
         react_pair(0, now)
+        twin_hop(step, now).start()
+        twin_strip_hop(step, now).start()
 
     advance(1)
     advance(2)
+    advance(3)
 
     def later(step, carry):
         advance(step)
         return carry
 
-    lax.fori_loop(3, STEPS, later, 0)
+    lax.fori_loop(4, STEPS, later, 0)
 
     last = (STEPS - 1) % 2
     middle_sums(tiles(last), strip_packed[last, 0], 1, move_plane, lambda total: None)
-    for way in ways:
-        for copy in (hop(way, HOPS - 1, 1 - last), strip_hop(way, HOPS - 1, 1 - last)):
-            receiving(ends_x, way, copy.wait_recv)
+    rim_action(hop(HOPS - 1, 1 - last).wait_recv)
+    rim_action(strip_hop(HOPS - 1, 1 - last).wait_recv)
     rim_step(STEPS - 1, 1 - last)
-    react_strip(1, last, every)
-    rim_planes(last)
+    react_strip(1, last, rim_lanes)
+    react_plane(9 * odd, last)
+    take_twin(STEPS - 1, last)
     edge_sums(tiles(last), strips_of(last), move_plane, None)
     corner_sent(0)
     corner_sent(1)
+    rim_action(hop(HOPS - 1, 1 - last).wait_send)
+    rim_action(strip_hop(HOPS - 1, 1 - last).wait_send)
+    for step, parity in ((HOPS - 1, 1 - last), (HOPS, last)):
+        twin_hop(step, parity).wait_send()
+        twin_strip_hop(step, parity).wait_send()
     for way in ways:
-        for copy in (hop(way, HOPS - 1, 1 - last), strip_hop(way, HOPS - 1, 1 - last)):
-            sending(ends_x, way, copy.wait_send)
         sending(ends_y, way, early[way].wait_send)
         sending(ends_y, way, late[way].wait_send)
 
@@ -874,11 +932,12 @@
             vmem((2, 2, 16, 128), f32),
             vmem((2, 16, 128), f32),
             vmem((2, 16, 128), f32),
-            vmem((16, 128), f32),
-            vmem((2, 4, 16, 128), f32),
+            vmem((2, 2, 16, 128), f32),
             vmem((9, 16, 128), f32),
-            vmem((2, HOPS, 16, 256), f32),
-            vmem((2, HOPS, 16, 128), f32),
+            vmem((HOPS, 16, 256), f32),
+            vmem((HOPS, 16, 128), f32),
+            vmem((STEPS, 16, 256), f32),
+            vmem((STEPS, 16, 128), f32),
             vmem((2, 16, 128), f32),
             vmem((16, 128), f32),
             vmem((2, 16, 128), f32),
@@ -888,10 +947,14 @@
             vmem((2, 2, 16, 128), f32),
             vmem((2, 16, 256), f32),
             vmem((2, 2, 16, 256), f32),
-            sems((2, HOPS)),
-            sems((2, HOPS)),
-            sems((2, HOPS)),
-            sems((2, HOPS)),
+            sems((HOPS,)),
+            sems((HOPS,)),
+            sems((HOPS,)),
+            sems((HOPS,)),
+            sems((STEPS,)),
+            sems((STEPS,)),
+            sems((STEPS,)),
+            sems((STEPS,)),
             sems((4, 2)),
             sems((4, 2)),
             sems((2, 2)),

time: 37 us -> 36.4 us (0.984)
  the two profiles are of different devices: /device:TPU:91 before, /device:TPU:199 now
where the time goes in v4:
time: 36.4 us; the launch traced here: 36.3 us
  Pallas kernels  36.3 us (100%)
    pallas_call x1, Pallas kernels, shards(): pl.pallas_call(kernel, out_shape=vmem((COMPS, 10, 16, 256), f32), in_spec...  35 us
    pallas_call x1, Pallas kernels, shards(): pl.pallas_call(unload, out_shape=jax.ShapeDtypeStruct(state.shape, f32),...  1.23 us

profile of v4, /device:TPU:199, one launch (start us, length us, event | category | flops | bytes accessed | tf_op | source)
XLA Modules:
  0.0 36.3 jit_solution(17859684760061309288)
XLA Ops:
  0.0 35.0 %slab.1.cells = f32[12,10,16,256]{3,2,1,0:T(8,128)S(1)} custom-call(f32[12,8,16,256]{3,2,1,0:T(8,128)} %state_ref.1, s32[8,2,16]{2,1,0:T(2,128)} %bitcast.1, s32[16]{0:T(128)} %layer_ref.1, f32[2,8]{1,0:T(2,128)} %fibre_ref.1), custom_call_target="tpu_custom_call" | custom-call | tf_op jit(solution)/shard_map/slab/pallas_call | solution.py:917
  35.0 1.2 %unload.1 = f32[12,8,16,256]{3,2,1,0:T(8,128)} custom-call(f32[12,10,16,256]{3,2,1,0:T(8,128)S(1)} %slab.1.cells), custom_call_target="tpu_custom_call" | custom-call | tf_op jit(solution)/shard_map/unload/pallas_call | solution.py:969

commit v5 on v4

--- a/solution.py
+++ b/solution.py
@@ -567,14 +567,14 @@
     for way in ways:
         sending(ends_y, way, early[way].start)
     rim_action(rim_copy(0).start)
-    rim_action(rim_copy(1).start)
     for way in ways:
         sending(ends_x, way, lead[way].start)
     twin_hop(0, 0).start()
     for way in ways:
         sending(ends_y, way, late[way].start)
+    rim_action(rim_copy(2).start)
     corner_start(1)
-    rim_action(rim_copy(2).start)
+    rim_action(rim_copy(1).start)
 
     def unpack(index):
         one = jnp.where(inner_half, side_in[0, index], side_in[1, index])
@@ -745,7 +745,6 @@
         for way in ways:
             receiving(ends_x, way, lead[way].wait_recv)
         rim_action(rim_copy(0).wait_recv)
-        rim_action(rim_copy(1).wait_recv)
         twin_hop(0, 0).wait_recv()
         moved = []
         outer_mask = jnp.zeros((16, 128), jnp.float32)
@@ -781,6 +780,7 @@
 
     def open_rim_gates():
         corner_wait(1)
+        rim_action(rim_copy(1).wait_recv)
         rim_action(rim_copy(2).wait_recv)
         for half, gates in enumerate((range(1, 9), range(9, 12))):
             for group, comp in enumerate(gates):

time: 36.4 us -> 37 us (1.016)
  the two profiles are of different devices: /device:TPU:199 before, /device:TPU:225 now
where the time goes in v5:
time: 37 us; the launch traced here: 36.9 us
  Pallas kernels  36.9 us (100%)
    pallas_call x1, Pallas kernels, shards(): pl.pallas_call(kernel, out_shape=vmem((COMPS, 10, 16, 256), f32), in_spec...  35.7 us
    pallas_call x1, Pallas kernels, shards(): pl.pallas_call(unload, out_shape=jax.ShapeDtypeStruct(state.shape, f32),...  1.23 us

profile of v5, /device:TPU:225, one launch (start us, length us, event | category | flops | bytes accessed | tf_op | source)
XLA Modules:
  0.0 36.9 jit_solution(5005120082072155814)
XLA Ops:
  0.0 35.7 %slab.1.cells = f32[12,10,16,256]{3,2,1,0:T(8,128)S(1)} custom-call(f32[12,8,16,256]{3,2,1,0:T(8,128)} %state_ref.1, s32[8,2,16]{2,1,0:T(2,128)} %bitcast.1, s32[16]{0:T(128)} %layer_ref.1, f32[2,8]{1,0:T(2,128)} %fibre_ref.1), custom_call_target="tpu_custom_call" | custom-call | tf_op jit(solution)/shard_map/slab/pallas_call | solution.py:917
  35.7 1.2 %unload.1 = f32[12,8,16,256]{3,2,1,0:T(8,128)} custom-call(f32[12,10,16,256]{3,2,1,0:T(8,128)S(1)} %slab.1.cells), custom_call_target="tpu_custom_call" | custom-call | tf_op jit(solution)/shard_map/unload/pallas_call | solution.py:969
